TPU v7x, 256 devices: a whole 4x4x8 slice. The times are simulated.
256 devices in a mesh: seq: 16 (over z, core), head: 16 (over x, y).
Axes of the slice: x: 4, y: 4, z: 8, core: 2. Of those that a mesh axis runs over, the one named last changes fastest.
Arguments:
- queries: bfloat16 [8192, 4096], P('seq', 'head'), may hold values from -6 to 6
- keys: bfloat16 [8192, 1024], P(('seq', 'head')), may hold values from -6 to 6
- values: bfloat16 [8192, 1024], P(('seq', 'head')), may hold values from -3 to 3
- attn_out: bfloat16 [8192, 4096], P('seq', 'head'), may hold values from -1.796875 to 1.796875
- out_grad: bfloat16 [8192, 4096], P('seq', 'head'), may hold values from -6 to 6
- log_norm: float32 [32, 8192], P('head', 'seq'), may hold values from 3.5 to 5.5
- block_layout: int32 [32, 64, 64], P('head'), may hold values 0 or 1
- document_ids: int32 [8192], replicated, may hold values from 0 to 7, never falling along the last dimension, each value on 1 to 4096 neighbouring positions
- block_order: int32 [64], replicated, may hold values from 0 to 63, each once
Outputs:
- query_grad: float32 [8192, 4096], P('seq', 'head')
- key_grad: float32 [8192, 1024], P(('seq', 'head'))
- value_grad: float32 [8192, 1024], P(('seq', 'head'))
Inputs may be any that keep to these rules, and one draw needn't show every extreme that they name: `document_ids`: never falls along the sequence position; each document covers 1 to 4096 positions, one exactly 4096. `block_order`: each sequence block once.
All inputs are finite; a program needn't handle non-finite values.
Results may differ from a plain program's by a relative error of at most 0.0029.
Values may be sent and summed in bfloat16 or wider, within the bound.
A program may use at most 128 MiB of HBM per device.

v0:
```python
import jax
import jax.numpy as jnp
from jax import lax
from jax.sharding import PartitionSpec as P

D_HEAD = 128
GROUP = 4
BLOCK = 128


def in_one_piece(arrays, axis, dim, along):
    both = jnp.concatenate(arrays, axis=along)
    result, at, gathered = (lax.all_gather(both, axis, axis=dim, tiled=True), 0, [])
    for a in arrays:
        gathered.append(lax.slice_in_dim(result, at, at + a.shape[along], axis=along))
        at += a.shape[along]
    return tuple(gathered)


def side_by_side(arrays, axis, dim, along):
    both = jnp.concatenate(arrays, axis=along)
    result, at, gathered = (lax.psum_scatter(both, axis, scatter_dimension=dim, tiled=True), 0, [])
    for a in arrays:
        gathered.append(lax.slice_in_dim(result, at, at + a.shape[along], axis=along))
        at += a.shape[along]
    return tuple(gathered)


def lookup_rows(first_row, count, block_order, document_ids):
    stored = first_row + jnp.arange(count, dtype=jnp.int32)
    blocks = stored // BLOCK
    table = jnp.arange(block_order.shape[0], dtype=jnp.int32)
    matches = blocks[:, None] == table[None, :]
    placed = jnp.sum(jnp.where(matches, block_order[None, :], 0), axis=1)
    position = placed * BLOCK + stored % BLOCK
    placed_hit = (placed[:, None] == table[None, :]).astype(jnp.float32)
    return (position, jnp.take(document_ids, position), placed_hit)


def body(
    queries, keys, values, attn_out, out_grad, log_norm, block_layout, document_ids, block_order
):
    tok_rows = queries.shape[0]
    head_count = log_norm.shape[0]
    head_width = D_HEAD
    kv_total = keys.shape[1] // head_width
    repeats = GROUP // head_count
    seq_size = lax.axis_size("seq")
    own_index = lax.axis_index("seq")
    scaling = head_width ** (-0.5)

    def widen(source):
        shaped = source.reshape(source.shape[0], kv_total, 1, head_width)
        shaped = jnp.broadcast_to(shaped, (source.shape[0], kv_total, repeats, head_width))
        return shaped.reshape(source.shape[0], kv_total * repeats * head_width)

    own_keys, own_values = (
        lax.all_to_all(widen(keys), "head", split_axis=1, concat_axis=0, tiled=True),
        lax.all_to_all(widen(values), "head", split_axis=1, concat_axis=0, tiled=True),
    )
    query_pos, query_docs, query_hit = lookup_rows(
        own_index * tok_rows, tok_rows, block_order, document_ids
    )
    query_heads = queries.reshape(tok_rows, head_count, head_width)
    grad_heads = out_grad.reshape(tok_rows, head_count, head_width)
    out_heads = attn_out.reshape(tok_rows, head_count, head_width)
    delta_rows = jnp.einsum(
        "qhd,qhd->hq", grad_heads, out_heads, preferred_element_type=jnp.float32
    )
    layout_rows = jnp.einsum("qa,hab->hqb", query_hit, block_layout.astype(jnp.float32))

    def block_grads(key_block, value_block, first_row):
        key_pos, key_docs, key_hit = lookup_rows(
            first_row, key_block.shape[0], block_order, document_ids
        )
        reach = jnp.einsum("hqb,kb->hqk", layout_rows, key_hit) > 0.5
        same_doc = (query_docs[:, None] == key_docs[None, :]) & (
            key_pos[None, :] <= query_pos[:, None]
        )
        reach = reach & same_doc[None, :, :]
        scores = (
            jnp.einsum("qhd,kd->hqk", query_heads, key_block, preferred_element_type=jnp.float32)
            * scaling
        )
        weights = jnp.where(reach, jnp.exp(scores - log_norm[:, :, None]), 0.0)
        weights_low = weights.astype(jnp.bfloat16)
        value_part = jnp.einsum(
            "hqk,qhd->kd", weights_low, grad_heads, preferred_element_type=jnp.float32
        )
        grad_scores = jnp.einsum(
            "qhd,kd->hqk", grad_heads, value_block, preferred_element_type=jnp.float32
        )
        score_grad = (weights * (grad_scores - delta_rows[:, :, None])).astype(jnp.bfloat16)
        query_part = jnp.einsum(
            "hqk,kd->qhd", score_grad, key_block, preferred_element_type=jnp.float32
        )
        key_part = jnp.einsum(
            "hqk,qhd->kd", score_grad, query_heads, preferred_element_type=jnp.float32
        )
        return (query_part, key_part, value_part)

    zero_query = jnp.zeros((tok_rows, head_count, head_width), jnp.float32)
    total_rows = tok_rows * seq_size
    zero_sums = jnp.zeros((total_rows, head_width), jnp.float32)
    piece_keys, piece_values = in_one_piece((own_keys, own_values), "seq", 0, 1)
    count = piece_keys.shape[0] // tok_rows

    def inner(sub_index, inner_totals):
        query_sum, key_sums, value_sums = inner_totals
        first_row = sub_index * tok_rows
        sub_keys = lax.dynamic_slice_in_dim(piece_keys, sub_index * tok_rows, tok_rows, 0)
        sub_values = lax.dynamic_slice_in_dim(piece_values, sub_index * tok_rows, tok_rows, 0)
        query_part, key_part, value_part = block_grads(sub_keys, sub_values, first_row)
        key_old = lax.dynamic_slice_in_dim(key_sums, first_row, tok_rows, 0)
        value_old = lax.dynamic_slice_in_dim(value_sums, first_row, tok_rows, 0)
        key_sums = lax.dynamic_update_slice_in_dim(key_sums, key_old + key_part, first_row, 0)
        value_sums = lax.dynamic_update_slice_in_dim(
            value_sums, value_old + value_part, first_row, 0
        )
        return (query_sum + query_part, key_sums, value_sums)

    query_total, key_sums, value_sums = lax.fori_loop(
        0, count, inner, (zero_query, zero_sums, zero_sums)
    )
    key_total, value_total = side_by_side((key_sums, value_sums), "seq", 0, 1)
    key_scaled = key_total * scaling
    key_merged, value_merged = (
        lax.all_to_all(key_scaled, "head", split_axis=0, concat_axis=1, tiled=True),
        lax.all_to_all(value_total, "head", split_axis=0, concat_axis=1, tiled=True),
    )

    def fold_pairs(merged):
        row_count = merged.shape[0]
        return (
            merged.reshape(row_count, kv_total, repeats, head_width)
            .sum(axis=2)
            .reshape(row_count, kv_total * head_width)
        )

    query_grad = (query_total * scaling).reshape(tok_rows, head_count * head_width)
    return (query_grad, fold_pairs(key_merged), fold_pairs(value_merged))


def solution(mesh):
    in_specs = (
        P("seq", "head"),
        P(("seq", "head"), None),
        P(("seq", "head"), None),
        P("seq", "head"),
        P("seq", "head"),
        P("head", "seq"),
        P("head", None, None),
        P(),
        P(),
    )
    out_specs = (P("seq", "head"), P(("seq", "head"), None), P(("seq", "head"), None))
    return jax.shard_map(body, mesh=mesh, in_specs=in_specs, out_specs=out_specs, check_vma=False)
```

profile of v0, /device:TPU:1, one launch (start us, length us, event | category | flops | bytes accessed | tf_op | source)
XLA Modules:
  0.0 367.8 jit_solution(5688010881916700041)
XLA Ops:
  8.7 7.6 %all-to-all-start = ((bf16[32,16,128]{2,0,1:T(8,128)(2,1)}), bf16[32,16,128]{2,0,1:T(8,128)(2,1)S(1)}, u32[]{:S(2)}, u32[]{:S(2)}) async-start(bf16[32,16,128]{2,0,1:T(8,128)(2,1)} %bitcast.2), calls=%async_computation | async-start | bytes 262144 | tf_op jit(solution)/shard_map/all_to_all | solution.py:58
  17.2 5.9 %all-to-all-done = bf16[32,16,128]{2,0,1:T(8,128)(2,1)S(1)} async-done(((bf16[32,16,128]{2,0,1:T(8,128)(2,1)}), bf16[32,16,128]{2,0,1:T(8,128)(2,1)S(1)}, u32[]{:S(2)}, u32[]{:S(2)}) %all-to-all-start) | async-done | bytes 131104 | tf_op jit(solution)/shard_map/all_to_all | solution.py:58
  23.2 10.0 %all_to_all.70 = bf16[32,16,128]{2,0,1:T(8,128)(2,1)S(1)} all-to-all(bf16[32,16,128]{2,0,1:T(8,128)(2,1)S(1)} %bitcast.143), channel_id=1, replica_groups=mesh['seq'=16,'head'=16] {'head'}, dimensions={1} | all-to-all | bytes 262144 | tf_op jit(solution)/shard_map/all_to_all | solution.py:59
  37.0 3.1 gather_fusion.1
  40.2 38.2 %all-gather.2.cloned.1.call-done = bf16[8192,256]{1,0:T(8,128)(2,1)} async-done(((bf16[512,256]{1,0:T(8,128)(2,1)}), bf16[8192,256]{1,0:T(8,128)(2,1)}) %all-gather.2.cloned.1.call-update) | async-done | bytes 4194320 | tf_op jit(solution)/shard_map/all_gather | solution.py:13
  78.4 3.8 %fusion.35 = (bf16[8192,128]{1,0:T(8,128)(2,1)}, bf16[8192,128]{1,0:T(8,128)(2,1)S(1)}) fusion(bf16[8192,256]{1,0:T(8,128)(2,1)} %all-gather.2.cloned.1.call-done), kind=kLoop, calls=%fused_computation.78 | loop fusion | bytes 8388608 | tf_op jit(solution)/shard_map/slice | solution.py:15
  86.7 173.5 %while.20 = (s32[]{:T(128)}, f32[512,2,128]{0,2,1:T(8,128)S(1)}, f32[8192,128]{1,0:T(8,128)}, f32[8192,128]{1,0:T(8,128)}, bf16[8192,128]{1,0:T(8,128)(2,1)S(1)}...) while((s32[]{:T(128)}, f32[512,2,128]{0,2,1:T(8,128)S(1)}, ...), condition=%wide.region_3.5_spmd.clone, body=%wide.region_1.4_spmd.clone.sunk | while | flops 744247808 | bytes 17875464 | solution.py:122
  86.8 3.1 gather_fusion
  97.7 3.1 gather_fusion
  119.4 3.1 gather_fusion
  130.3 3.1 gather_fusion
  141.1 3.1 gather_fusion
  162.8 3.1 gather_fusion
  173.6 3.1 gather_fusion
  206.1 3.1 gather_fusion
  227.8 3.1 gather_fusion
  238.6 3.1 gather_fusion
  249.5 3.1 gather_fusion
  260.2 7.2 %pad_maximum_fusion = f32[8192,256]{1,0:T(8,128)} fusion(f32[8192,128]{1,0:T(8,128)} %get-tuple-element.363, f32[8192,128]{1,0:T(8,128)} %get-tuple-element.362), kind=kLoop, calls=%fused_computation.48 | loop fusion | flops 2097152 | bytes 16777216 | tf_op jit(solution)/shard_map/concatenate | solution.py:21
  267.5 66.1 %reduce-scatter.2.cloned.1.call-done = f32[512,256]{1,0:T(8,128)} async-done(((f32[8192,256]{1,0:T(8,128)}), f32[512,256]{1,0:T(8,128)}) %reduce-scatter.2.cloned.1.call-update) | async-done | bytes 524304 | tf_op jit(solution)/shard_map/reduce_scatter | solution.py:22
  335.4 6.7 %all-to-all-start.2 = ((f32[16,32,128]{2,1,0:T(8,128)}), f32[16,32,128]{2,1,0:T(8,128)S(1)}, u32[]{:S(2)}, u32[]{:S(2)}) async-start(f32[16,32,128]{2,1,0:T(8,128)} %bitcast.17), calls=%async_computation.3 | async-start | bytes 524288 | tf_op jit(solution)/shard_map/all_to_all | solution.py:128
  343.2 6.3 %all-to-all-done.2 = f32[16,32,128]{2,1,0:T(8,128)S(1)} async-done(((f32[16,32,128]{2,1,0:T(8,128)}), f32[16,32,128]{2,1,0:T(8,128)S(1)}, u32[]{:S(2)}, u32[]{:S(2)}) %all-to-all-start.2) | async-done | bytes 262176 | tf_op jit(solution)/shard_map/all_to_all | solution.py:128
  349.4 3.5 all-to-all-start.3
  353.7 6.6 %all-to-all-done.3 = f32[16,32,128]{2,1,0:T(8,128)S(1)} async-done(((f32[16,32,128]{2,1,0:T(8,128)}), f32[16,32,128]{2,1,0:T(8,128)S(1)}, u32[]{:S(2)}, u32[]{:S(2)}) %all-to-all-start.3) | async-done | bytes 262176 | tf_op jit(solution)/shard_map/all_to_all | solution.py:129
  (247 shorter events, 152.9 us)
Async XLA Ops:
  7.2 0.8 copy-start
  7.2 27.8 %copy-start.6 = (s32[64]{0:T(128)S(1)}, s32[64]{0:T(128)}, u32[]{:S(2)}) copy-start(s32[64]{0:T(128)} %param.21) | copy-start | bytes 772
  7.2 28.1 %copy-start.2 = (bf16[512,256]{1,0:T(8,128)(2,1)S(1)}, bf16[512,256]{1,0:T(8,128)(2,1)}, u32[]{:S(2)}) copy-start(bf16[512,256]{1,0:T(8,128)(2,1)} %param.17) | copy-start | bytes 786436
  7.2 28.4 %copy-start.3 = (bf16[512,256]{1,0:T(8,128)(2,1)S(1)}, bf16[512,256]{1,0:T(8,128)(2,1)}, u32[]{:S(2)}) copy-start(bf16[512,256]{1,0:T(8,128)(2,1)} %param.13) | copy-start | bytes 786436
  8.7 14.4 %all-to-all-start = ((bf16[32,16,128]{2,0,1:T(8,128)(2,1)}), bf16[32,16,128]{2,0,1:T(8,128)(2,1)S(1)}, u32[]{:S(2)}, u32[]{:S(2)}) async-start(bf16[32,16,128]{2,0,1:T(8,128)(2,1)} %bitcast.2), calls=%async_computation | async-start | bytes 262144 | tf_op jit(solution)/shard_map/all_to_all | solution.py:58
  16.3 62.1 %all-gather.2.cloned.1.call-start = ((), (), s32[]{:S(2)}) async-start(), calls=%async_computation.5 | async-start | bytes 4456448 | tf_op jit(solution)/shard_map/all_gather | solution.py:13
  17.2 18.8 %copy-start.4 = (bf16[512,256]{1,0:T(8,128)(2,1)S(1)}, bf16[512,256]{1,0:T(8,128)(2,1)}, u32[]{:S(2)}) copy-start(bf16[512,256]{1,0:T(8,128)(2,1)} %param.16) | copy-start | bytes 786436
  33.9 299.6 %reduce-scatter.2.cloned.1.call-start = ((), (), s32[]{:S(2)}) async-start(), calls=%async_computation.6 | async-start | bytes 8912896 | tf_op jit(solution)/shard_map/reduce_scatter | solution.py:22
  35.4 1.6 copy-start.1
  84.4 2.2 copy-start.5
  335.4 14.0 %all-to-all-start.2 = ((f32[16,32,128]{2,1,0:T(8,128)}), f32[16,32,128]{2,1,0:T(8,128)S(1)}, u32[]{:S(2)}, u32[]{:S(2)}) async-start(f32[16,32,128]{2,1,0:T(8,128)} %bitcast.17), calls=%async_computation.3 | async-start | bytes 524288 | tf_op jit(solution)/shard_map/all_to_all | solution.py:128
  349.4 10.8 %all-to-all-start.3 = ((f32[16,32,128]{2,1,0:T(8,128)}), f32[16,32,128]{2,1,0:T(8,128)S(1)}, u32[]{:S(2)}, u32[]{:S(2)}) async-start(f32[16,32,128]{2,1,0:T(8,128)} %bitcast.20), calls=%async_computation.4 | async-start | bytes 524288 | tf_op jit(solution)/shard_map/all_to_all | solution.py:129
Sparse Core Ops, SparseCore 0:
  34.0 44.3 all-gather.1
  267.6 65.9 reduce-scatter.1
where the time goes:
time: 373 us; the launch traced here: 368 us
  waiting for transfers between devices  123 us (33%)
  matrix products  116 us (31%)
  local copies, waits for them, and re-layouts  67.5 us (18%)
  other arithmetic  18.2 us (5%)
  starting transfers between devices  17.9 us (5%)
  between operations  14.3 us (4%)
  blocking collectives  9.99 us (3%)
    reduce_scatter x1, waiting for transfers between devices, side_by_side(): lax.psum_scatter(both, axis, scatter_dimension=dim, tiled=True)  66.1 us
    gather x17, local copies, waits for them, and re-layouts, lookup_rows(): return (position, jnp.take(document_ids, position), placed_hit)  53.4 us
    all_gather x1, waiting for transfers between devices, in_one_piece(): lax.all_gather(both, axis, axis=dim, tiled=True)  38.2 us
    dot_general x16, matrix products, block_grads(): jnp.einsum('hqk,qhd->kd', weights_low, grad_heads, preferred_element_type...  33.7 us
    dot_general x16, matrix products, block_grads(): jnp.einsum('hqk,qhd->kd', score_grad, query_heads, preferred_element_type...  33.6 us
    dot_general x16, matrix products, block_grads(): jnp.einsum('qhd,kd->hqk', grad_heads, value_block, preferred_element_type...  21.6 us
    dot_general x16, matrix products, block_grads(): jnp.einsum('qhd,kd->hqk', query_heads, key_block, preferred_element_type=...  13.1 us
    all_to_all x1, blocking collectives, body(): lax.all_to_all(widen(values), 'head', split_axis=1, concat_axis=0, tiled=...  9.99 us
  transfers between devices with their start and end apart: 5, of which 5 were waited for; matrix products, arithmetic and copies ran while one was open for 2% of the time, Pallas kernels for 0%

commit v1 on v0

v1 whole, which is shorter than its diff:
```python
import functools

import jax
import jax.numpy as jnp
from jax import lax
from jax.experimental import pallas as pl
from jax.experimental.pallas import tpu as pltpu
from jax.sharding import PartitionSpec as P

MESH = pl.DeviceIdType.MESH
D = 128
GROUP = 4
BLOCK = 128
NBLK = 64
NZ = 8
TILE = 32
CHUNK_TILES = 4
CHUNK = TILE * CHUNK_TILES
KEYS = NBLK * TILE
PLANE_KEYS = KEYS // NZ
ROWS = 512
NEVER = 1e30
SCALE = D ** (-0.5)
BF16 = jnp.bfloat16
F32 = jnp.float32


def place():
    s = lax.axis_index("seq")
    h = lax.axis_index("head")
    return s, h, s // 2, s % 2, h // 4, h % 4


def send(src, dst, send_sem, recv_sem, seq, head):
    return pltpu.make_async_remote_copy(
        src_ref=src,
        dst_ref=dst,
        send_sem=send_sem,
        recv_sem=recv_sem,
        device_id=(seq, head),
        device_id_type=MESH,
    )


def greet(sources, count):
    barrier = pltpu.get_barrier_semaphore()
    for seq, head, other in sources:
        if other is None:
            pl.semaphore_signal(barrier, inc=1, device_id=(seq, head), device_id_type=MESH)
        else:

            @pl.when(other)
            def _():
                pl.semaphore_signal(barrier, inc=1, device_id=(seq, head), device_id_type=MESH)

    pl.semaphore_wait(barrier, count)


SUBS = ((0, 0), (0, 1), (1, 0), (1, 1))
HALF = PLANE_KEYS // 2


def gather_kernel(
    keys, values, queries, grads, outs, norms, layout,
    kv_all, q_all, g_all, s_all, l_all,
    stats, a_send, a_recv, z_send, z_recv, y_send, y_recv, d_send, d_recv, f_send, f_recv,
):
    s, h, z, c, x, y = place()
    pair = h + 1 - 2 * (y % 2)
    twin = s + 1 - 2 * c
    up = ((z + 1) % NZ) * 2 + c
    down = ((z + NZ - 1) % NZ) * 2 + c
    hp = y % 2
    quarter = hp * 2 + c

    takers = []
    for xg in range(4):
        for yp in range(2):
            seq, head = z * 2 + y % 2, xg * 4 + yp * 2 + y // 2
            takers.append((seq, head, (seq != s) | (head != h)))
    givers = []
    for cg in range(2):
        for xg in range(4):
            seq, head = z * 2 + cg, xg * 4 + quarter
            givers.append((seq, head, (seq != s) | (head != h)))
    own = ((y % 2 == c) & (y // 2 == hp)).astype(jnp.int32)
    greet(
        [(s, pair, None), (twin, h, None), (up, h, None), (down, h, None)] + givers,
        4 + 8 - own,
    )

    slot = c * 4 + x
    a_copies = []
    for g, (seq, head, other) in enumerate(takers):
        for t, src in enumerate((keys, values)):
            copy = send(
                src.at[:, pl.ds(g * D, D)],
                kv_all.at[t, z, pl.ds(pl.multiple_of(slot * TILE, TILE), TILE), :],
                a_send.at[t, g],
                a_recv.at[t, slot],
                seq,
                head,
            )
            pl.when(other)(copy.start)
            a_copies.append((copy, other))

            @pl.when(jnp.logical_not(other))
            def _():
                kv_all[t, z, pl.ds(pl.multiple_of(slot * TILE, TILE), TILE), :] = src[:, g * D : (g + 1) * D]

    y_copies = [
        send(queries, q_all.at[c, hp], y_send.at[0], y_recv.at[0], s, pair),
        send(grads, g_all.at[c, hp], y_send.at[1], y_recv.at[1], s, pair),
        send(layout, l_all.at[hp], y_send.at[2], y_recv.at[2], s, pair),
        send(stats, s_all.at[c, hp], y_send.at[3], y_recv.at[3], s, pair),
    ]
    d_copies = [
        send(queries, q_all.at[c, hp], d_send.at[0], d_recv.at[0], twin, h),
        send(grads, g_all.at[c, hp], d_send.at[1], d_recv.at[1], twin, h),
        send(stats, s_all.at[c, hp], d_send.at[2], d_recv.at[2], twin, h),
    ]
    for copy in y_copies[:2] + d_copies[:2]:
        copy.start()

    ones = jnp.ones((8, D), BF16)
    for hh in range(2):
        stats[hh * 4 : hh * 4 + 4, :] = norms[hh * 4 : hh * 4 + 4, :]
        for rb in range(4):
            at = (slice(rb * BLOCK, (rb + 1) * BLOCK), slice(hh * D, (hh + 1) * D))
            product = grads[at].astype(F32) * outs[at].astype(F32)
            high = product.astype(BF16)
            low = (product - high.astype(F32)).astype(BF16)
            dims = (((1,), (1,)), ((), ()))
            total = lax.dot_general(ones, high, dims, preferred_element_type=F32)
            total = total + lax.dot_general(ones, low, dims, preferred_element_type=F32)
            stats[8 + hh * 4 + rb : 9 + hh * 4 + rb, :] = total[0:1, :]
    for copy in (y_copies[2], y_copies[3], d_copies[2]):
        copy.start()
    s_all[c, hp] = stats[...]
    l_all[hp] = layout[...]
    q_all[c, hp] = queries[...]
    g_all[c, hp] = grads[...]

    def piece(t, half, plane):
        return kv_all.at[t, plane, pl.ds(half * HALF, HALF), :]

    def hop(way, step, sub):
        t, half = SUBS[sub]
        origin = (z + NZ - (step - 1)) % NZ if way == 0 else (z + step - 1) % NZ
        return send(
            piece(t, half, origin), piece(t, half, origin),
            z_send.at[way, step - 1, sub], z_recv.at[way, step - 1, sub],
            up if way == 0 else down, h,
        )

    def carries(way, step, sub):
        return step < 4 or (step == 4 and SUBS[sub][0] == way)

    z_copies = {}
    for sub, (t, half) in enumerate(SUBS):
        for k in range(4):
            at = half * 4 + k
            seq, head, other = givers[at]
            landed = send(
                keys.at[:, pl.ds(0, D)], kv_all.at[t, z, pl.ds(at * TILE, TILE), :],
                a_send.at[t, 0], a_recv.at[t, at], seq, head,
            )
            pl.when(other)(landed.wait_recv)
        for way in range(2):
            z_copies[way, 1, sub] = hop(way, 1, sub)
            z_copies[way, 1, sub].start()

    forwards = []

    def pass_on(k, ref_all):
        y_copies[k].wait_recv()
        copy = send(ref_all.at[c, 1 - hp], ref_all.at[c, 1 - hp], f_send.at[len(forwards)], f_recv.at[len(forwards)], twin, h)
        copy.start()
        forwards.append(copy)

    for step in range(1, 5):
        for sub in range(4):
            for way in range(2):
                if not carries(way, step, sub):
                    continue
                z_copies[way, step, sub].wait_recv()
                if carries(way, step + 1, sub):
                    z_copies[way, step + 1, sub] = hop(way, step + 1, sub)
                    z_copies[way, step + 1, sub].start()
        if step == 1:
            pass_on(0, q_all)
        if step == 3:
            pass_on(1, g_all)
            pass_on(3, s_all)
            y_copies[2].wait_recv()

    for copy in d_copies + forwards:
        copy.wait_recv()
    for copy, other in a_copies:
        pl.when(other)(copy.wait_send)
    for copy in list(z_copies.values()) + y_copies + d_copies + forwards:
        copy.wait_send()


def gather(keys, values, queries, grads, outs, norms, layout):
    vmem = pl.BlockSpec(memory_space=pltpu.VMEM)
    dma = pltpu.SemaphoreType.DMA
    return pl.pallas_call(
        gather_kernel,
        name="exchange_in",
        out_shape=(
            jax.ShapeDtypeStruct((2, NZ, PLANE_KEYS, D), BF16),
            jax.ShapeDtypeStruct((2, 2, ROWS, 2 * D), BF16),
            jax.ShapeDtypeStruct((2, 2, ROWS, 2 * D), BF16),
            jax.ShapeDtypeStruct((2, 2, 16, BLOCK), F32),
            jax.ShapeDtypeStruct((2, 2 * NBLK, NBLK), BF16),
        ),
        in_specs=[vmem] * 7,
        out_specs=(vmem,) * 5,
        scratch_shapes=[
            pltpu.VMEM((16, BLOCK), F32),
            dma((2, 8)), dma((2, 8)),
            dma((2, 4, 4)), dma((2, 4, 4)),
            dma((4,)), dma((4,)),
            dma((3,)), dma((3,)),
            dma((3,)), dma((3,)),
        ],
        compiler_params=pltpu.CompilerParams(collective_id=0, has_side_effects=True),
    )(keys, values, queries, grads, outs, norms, layout)


def attend_kernel(
    where_ref, order, first, kv, q_all, g_all, s_all, l_all, start,
    dq, dkv,
    ks, vs, dks, dvs, lay, pick, bias, qs, gs, dqt,
):
    z, quarter = where_ref[0], where_ref[1]

    def sort(sb, _):
        to = pl.ds(pl.multiple_of(order[sb] * TILE, TILE), TILE)
        at = pl.ds(pl.multiple_of(sb * TILE, TILE), TILE)
        ks[to, :] = kv[0, at, :]
        vs[to, :] = kv[1, at, :]
        return 0

    lax.fori_loop(0, NBLK, sort, 0, unroll=8)
    dks[...] = jnp.zeros_like(dks)
    dvs[...] = jnp.zeros_like(dvs)
    for hp in range(2):
        lay[hp * 2 * NBLK : (hp + 1) * 2 * NBLK, :] = l_all[hp].astype(F32)
    pick[...] = jnp.zeros_like(pick)
    spread = (
        lax.broadcasted_iota(jnp.int32, (8, GROUP * BLOCK), 1) // BLOCK
        == lax.broadcasted_iota(jnp.int32, (8, GROUP * BLOCK), 0)
    ).astype(F32)
    nt = (((1,), (1,)), ((), ()))
    tn = (((0,), (0,)), ((), ()))
    row = lax.broadcasted_iota(jnp.int32, (TILE, GROUP * BLOCK), 0)

    def one_block(i, _):
        cb, rb = i // 4, i % 4
        block = order[z * 8 + i]
        rows = pl.ds(pl.multiple_of(rb * BLOCK, BLOCK), BLOCK)
        norm, delta = [], []
        for head in range(GROUP):
            hp, hh = head // 2, head % 2
            qs[head * BLOCK : (head + 1) * BLOCK, :] = q_all[cb, hp, rows, hh * D : (hh + 1) * D]
            gs[head * BLOCK : (head + 1) * BLOCK, :] = g_all[cb, hp, rows, hh * D : (hh + 1) * D]
            norm.append(s_all[cb, hp, pl.ds(hh * 4 + rb, 1), :])
            delta.append(s_all[cb, hp, pl.ds(8 + hh * 4 + rb, 1), :])
            pick[head : head + 1, :] = lay[pl.ds(head * NBLK + block, 1), :]
        norm = jnp.concatenate(norm, axis=1)
        delta = jnp.concatenate(delta, axis=1)
        seen = lax.dot_general(pick[...], spread, tn, preferred_element_type=F32)
        bias[...] = jnp.where(seen > 0.5, norm, NEVER)
        begin = start[pl.ds(block, 1), :]
        begin = jnp.concatenate([begin] * GROUP, axis=1)
        last = block * BLOCK + lax.broadcasted_iota(jnp.int32, (1, GROUP * BLOCK), 1) % BLOCK
        dqt[...] = jnp.zeros_like(dqt)

        def one_chunk(ch, _):
            at = pl.ds(pl.multiple_of(ch * CHUNK, CHUNK), CHUNK)
            kc, vc = ks[at, :], vs[at, :]
            scores = lax.dot_general(kc, qs[...], nt, preferred_element_type=F32)
            grad_scores = lax.dot_general(vc, gs[...], nt, preferred_element_type=F32)
            low, score_grad = [], []
            for t in range(CHUNK_TILES):
                part = slice(t * TILE, (t + 1) * TILE)
                tile = ch * CHUNK_TILES + t
                position = row + (tile * BLOCK + quarter * TILE)
                visible = (position >= begin) & (position <= last)
                weights = jnp.exp(scores[part, :] * SCALE - bias[pl.ds(tile, 1), :])
                weights = jnp.where(visible, weights, 0.0)
                low.append(weights.astype(BF16))
                score_grad.append((weights * (grad_scores[part, :] - delta)).astype(BF16))
            low = jnp.concatenate(low, axis=0)
            score_grad = jnp.concatenate(score_grad, axis=0)
            dvs[at, :] += jnp.dot(low, gs[...], preferred_element_type=F32)
            dks[at, :] += jnp.dot(score_grad, qs[...], preferred_element_type=F32)
            dqt[...] += lax.dot_general(kc, score_grad, tn, preferred_element_type=F32)
            return 0

        lax.fori_loop(first[block] // CHUNK_TILES, block // CHUNK_TILES + 1, one_chunk, 0)
        for head in range(GROUP):
            hp, hh = head // 2, head % 2
            block_grad = dqt[:, head * BLOCK : (head + 1) * BLOCK].T
            dq[cb, hp, rows, hh * D : (hh + 1) * D] = block_grad * SCALE
        return 0

    lax.fori_loop(0, 8, one_block, 0)

    def unsort(sb, _):
        at = pl.ds(pl.multiple_of(order[sb] * TILE, TILE), TILE)
        to = pl.ds(pl.multiple_of(sb * TILE, TILE), TILE)
        dkv[0, to, :] = dks[at, :]
        dkv[1, to, :] = dvs[at, :]
        return 0

    lax.fori_loop(0, NBLK, unsort, 0, unroll=8)


def attend(where, order, first, kv, q_all, g_all, s_all, l_all, start):
    vmem = pl.BlockSpec(memory_space=pltpu.VMEM)
    smem = pl.BlockSpec(memory_space=pltpu.SMEM)
    return pl.pallas_call(
        attend_kernel,
        name="attend",
        out_shape=(
            jax.ShapeDtypeStruct((2, 2, ROWS, 2 * D), F32),
            jax.ShapeDtypeStruct((2, KEYS, D), F32),
        ),
        in_specs=[smem] * 3 + [vmem] * 6,
        out_specs=(vmem, vmem),
        scratch_shapes=[
            pltpu.VMEM((KEYS, D), BF16),
            pltpu.VMEM((KEYS, D), BF16),
            pltpu.VMEM((KEYS, D), F32),
            pltpu.VMEM((KEYS, D), F32),
            pltpu.VMEM((GROUP * NBLK, NBLK), F32),
            pltpu.VMEM((8, NBLK), F32),
            pltpu.VMEM((NBLK, GROUP * BLOCK), F32),
            pltpu.VMEM((GROUP * BLOCK, D), BF16),
            pltpu.VMEM((GROUP * BLOCK, D), BF16),
            pltpu.VMEM((D, GROUP * BLOCK), F32),
        ],
    )(where, order, first, kv, q_all, g_all, s_all, l_all, start)


def scatter_kernel(
    dq_part, dkv,
    dq, dk, dv,
    twin_in, pair_out, pair_in, z_out, z_in, fin, own_in,
    d_send, d_recv, y_send, y_recv, z_send, z_recv, a_send, a_recv,
):
    s, h, z, c, x, y = place()
    pair = h + 1 - 2 * (y % 2)
    twin = s + 1 - 2 * c
    up = ((z + 1) % NZ) * 2 + c
    down = ((z + NZ - 1) % NZ) * 2 + c
    hp = y % 2
    quarter = hp * 2 + c

    owners = []
    for cg in range(2):
        for xg in range(4):
            seq, head = z * 2 + cg, xg * 4 + quarter
            owners.append((seq, head, (seq != s) | (head != h)))
    makers = []
    for xg in range(4):
        for yp in range(2):
            seq, head = z * 2 + y % 2, xg * 4 + yp * 2 + y // 2
            makers.append((seq, head, (seq != s) | (head != h)))
    own = ((y % 2 == c) & (y // 2 == hp)).astype(jnp.int32)
    greet(
        [(s, pair, None), (twin, h, None), (up, h, None), (down, h, None)] + makers,
        4 + 8 - own,
    )

    d_copy = send(dq_part.at[1 - c], twin_in, d_send.at[0], d_recv.at[0], twin, h)
    d_copy.start()

    def rows_of(plane, half):
        return pl.ds(pl.multiple_of(plane * PLANE_KEYS + half * HALF, HALF), HALF)

    z_copies = {}

    def hop(way, step, sub):
        t, half = SUBS[sub]
        target = (z + 5 - step) % NZ if way == 0 else (z + NZ - (5 - step)) % NZ
        value = dkv[t, rows_of(target, half), :]
        if (way, step - 1, sub) in z_copies:
            z_copies[way, step - 1, sub].wait_recv()
            value = value + z_in[way, step - 2, sub].astype(F32)
        z_out[way, step - 1, sub] = value.astype(BF16)
        copy = send(
            z_out.at[way, step - 1, sub], z_in.at[way, step - 1, sub],
            z_send.at[way, step - 1, sub], z_recv.at[way, step - 1, sub],
            up if way == 0 else down, h,
        )
        copy.start()
        z_copies[way, step, sub] = copy

    for sub, (t, half) in enumerate(SUBS):
        hop(t, 1, sub)
    for sub, (t, half) in enumerate(SUBS):
        hop(1 - t, 2, sub)

    d_copy.wait_recv()
    pair_out[...] = (dq_part[c, 1 - hp] + twin_in[1 - hp]).astype(BF16)
    y_copy = send(pair_out, pair_in, y_send.at[0], y_recv.at[0], s, pair)
    y_copy.start()

    for sub, (t, half) in enumerate(SUBS):
        hop(t, 2, sub)
    dq[...] = dq_part[c, hp] + twin_in[hp]
    for step in (3, 4):
        for sub in range(4):
            for way in range(2):
                hop(way, step, sub)

    a_copies = []
    for half in range(2):
        for t in range(2):
            sub = t * 2 + half
            value = dkv[t, rows_of(z, half), :]
            for way in range(2):
                z_copies[way, 4, sub].wait_recv()
                value = value + z_in[way, 3, sub].astype(F32)
            if t == 0:
                value = value * SCALE
            for k in range(4):
                fin[half * 4 + k, t] = value[k * TILE : (k + 1) * TILE, :]
        for k in range(4):
            seq, head, other = owners[half * 4 + k]
            g = x * 2 + y // 2
            copy = send(
                fin.at[half * 4 + k], own_in.at[g],
                a_send.at[half * 4 + k], a_recv.at[g], seq, head,
            )
            pl.when(other)(copy.start)
            a_copies.append((copy, other))

            @pl.when(jnp.logical_not(other))
            def _():
                own_in[g] = fin[half * 4 + k]

    y_copy.wait_recv()
    dq[...] += pair_in[...].astype(F32)

    for g, (seq, head, other) in enumerate(makers):
        landed = send(fin.at[0], own_in.at[g], a_send.at[0], a_recv.at[g], seq, head)
        pl.when(other)(landed.wait_recv)
        dk[:, g * D : (g + 1) * D] = own_in[g, 0]
        dv[:, g * D : (g + 1) * D] = own_in[g, 1]

    for copy, other in a_copies:
        pl.when(other)(copy.wait_send)
    for copy in list(z_copies.values()) + [d_copy, y_copy]:
        copy.wait_send()


def scatter(dq_part, dkv):
    vmem = pl.BlockSpec(memory_space=pltpu.VMEM)
    dma = pltpu.SemaphoreType.DMA
    return pl.pallas_call(
        scatter_kernel,
        name="exchange_out",
        out_shape=(
            jax.ShapeDtypeStruct((ROWS, 2 * D), F32),
            jax.ShapeDtypeStruct((TILE, 8 * D), F32),
            jax.ShapeDtypeStruct((TILE, 8 * D), F32),
        ),
        in_specs=[vmem] * 2,
        out_specs=(vmem,) * 3,
        scratch_shapes=[
            pltpu.VMEM((2, ROWS, 2 * D), F32),
            pltpu.VMEM((ROWS, 2 * D), BF16),
            pltpu.VMEM((ROWS, 2 * D), BF16),
            pltpu.VMEM((2, 4, 4, HALF, D), BF16),
            pltpu.VMEM((2, 4, 4, HALF, D), BF16),
            pltpu.VMEM((8, 2, TILE, D), F32),
            pltpu.VMEM((8, 2, TILE, D), F32),
            dma((1,)), dma((1,)),
            dma((1,)), dma((1,)),
            dma((2, 4, 4)), dma((2, 4, 4)),
            dma((8,)), dma((8,)),
        ],
        compiler_params=pltpu.CompilerParams(collective_id=1, has_side_effects=True),
    )(dq_part, dkv)


def body(
    queries, keys, values, attn_out, out_grad, log_norm, block_layout, document_ids, block_order
):
    _, _, z, c, _, y = place()
    where = jnp.stack([z, (y % 2) * 2 + c]).astype(jnp.int32)
    below = jnp.sum(
        (document_ids[None, :] < jnp.arange(8, dtype=jnp.int32)[:, None]).astype(jnp.int32), axis=1
    )
    ids = document_ids.reshape(NBLK, BLOCK)
    start = jnp.zeros_like(ids)
    for d in range(1, 8):
        start = jnp.where(ids == d, below[d], start)
    first = start[:, 0] // BLOCK
    kv, q_all, g_all, s_all, l_all = gather(
        keys,
        values,
        queries,
        out_grad,
        attn_out,
        log_norm.reshape(8, BLOCK),
        block_layout.reshape(2 * NBLK, NBLK).astype(BF16),
    )
    dq_part, dkv = attend(
        where, block_order, first, kv.reshape(2, KEYS, D), q_all, g_all, s_all, l_all, start
    )
    return scatter(dq_part, dkv)


def solution(mesh):
    in_specs = (
        P("seq", "head"),
        P(("seq", "head"), None),
        P(("seq", "head"), None),
        P("seq", "head"),
        P("seq", "head"),
        P("head", "seq"),
        P("head", None, None),
        P(),
        P(),
    )
    out_specs = (P("seq", "head"), P(("seq", "head"), None), P(("seq", "head"), None))
    return jax.shard_map(body, mesh=mesh, in_specs=in_specs, out_specs=out_specs, check_vma=False)
```

time: 373 us -> 99 us (0.27); the launches traced: 368 us -> 98.1 us
  waiting for transfers between devices: 123 us -> 0 us
  matrix products: 116 us -> 0 us
  Pallas kernels: 0 us -> 81.6 us
  local copies, waits for them, and re-layouts: 67.5 us -> 7.09 us
  starting transfers between devices: 17.9 us -> 0 us
  between operations: 14.3 us -> 0.72 us
  blocking collectives: 9.99 us -> 0 us
  other arithmetic: 18.2 us -> 8.77 us
    dot_general x96 -> x0, matrix products: 116 us -> none  [the longest x16 33.7 us: block_grads(): jnp.einsum('hqk,qhd->kd', weights_low, grad_heads, preferred_element_type...]
    pallas_call x0 -> x3, Pallas kernels: none -> 81.6 us  [the longest x1 31.2 us: gather(): pl.pallas_call(gather_kernel, name='exchange_in', out_shape=(jax.ShapeDty...]
    reduce_scatter x1 -> x0, waiting for transfers between devices: 66.1 us -> none  [side_by_side(): lax.psum_scatter(both, axis, scatter_dimension=dim, tiled=True)]
    gather x17 -> x0, local copies, waits for them, and re-layouts: 53.4 us -> none  [lookup_rows(): return (position, jnp.take(document_ids, position), placed_hit)]
    all_gather x1 -> x0, waiting for transfers between devices: 38.2 us -> none  [in_one_piece(): lax.all_gather(both, axis, axis=dim, tiled=True)]
    all_to_all x3 -> x0, waiting for transfers between devices: 18.8 us -> none  [the longest x1 6.6 us: body(): lax.all_to_all(value_total, 'head', split_axis=0, concat_axis=1, tiled=True)]
    all_to_all x3 -> x0, starting transfers between devices: 17.8 us -> none  [the longest x1 7.57 us: body(): lax.all_to_all(widen(keys), 'head', split_axis=1, concat_axis=0, tiled=True)]
    all_to_all x1 -> x0, blocking collectives: 9.99 us -> none  [body(): lax.all_to_all(widen(values), 'head', split_axis=1, concat_axis=0, tiled=...]
  transfers between devices with their start and end apart: 5 -> 0, of which waited for: 5 -> 0; matrix products, arithmetic and copies ran while one was open for 2% -> 0% of each run, Pallas kernels for 0% -> 0%
where the time goes in v1:
time: 99 us; the launch traced here: 98.1 us
  Pallas kernels  81.6 us (82%)
  other arithmetic  8.77 us (9%)
  local copies, waits for them, and re-layouts  7.09 us (7%)
    pallas_call x1, Pallas kernels, gather(): pl.pallas_call(gather_kernel, name='exchange_in', out_shape=(jax.ShapeDty...  31.2 us
    pallas_call x1, Pallas kernels, scatter(): pl.pallas_call(scatter_kernel, name='exchange_out', out_shape=(jax.ShapeD...  30.3 us
    pallas_call x1, Pallas kernels, attend(): pl.pallas_call(attend_kernel, name='attend', out_shape=(jax.ShapeDtypeStr...  20 us
    select_n x1, other arithmetic, body(): start = jnp.where(ids == d, below[d], start)  5.19 us
    unnamed x5, local copies, waits for them, and re-layouts  5.01 us

profile of v1, /device:TPU:1, one launch (start us, length us, event | category | flops | bytes accessed | tf_op | source)
XLA Modules:
  0.0 98.1 jit_solution(10755257825155961083)
XLA Ops:
  0.7 0.6 pad_add_fusion.where_ref
  1.3 0.9 convert_reduce_fusion
  2.2 0.7 fusion
  2.9 1.3 %reshape.37.norms = f32[8,128]{1,0:T(8,128)} reshape(f32[2,512]{1,0:T(2,128)} %param.14) | data formatting | bytes 8192 | tf_op jit(solution)/shard_map/reshape | solution.py:511
  4.2 5.2 %select_bitcast_fusion.start = s32[64,128]{1,0:T(8,128)S(1)} fusion(s32[8192]{0:T(1024)} %param.16, s32[]{:T(128)} %bitcast.2, s32[]{:T(128)} %bitcast.3, s32[]{:T(128)} %bitcast.4, s32[]{:T(128)} %bitcast.5, s32[]{:T(128)} %bitcast.8, s32[]{:T(128)} %bitcast.7, s32[]{:T(128)} %bitcast.6), kind=kLoop, calls=%fused_computation.3 | loop fusion | flops 114688 | bytes 65564 | tf_op jit(solution)/shard_map/jit(_where)/select_n | solution.py:503
  9.4 0.0 copy-start
  9.4 0.1 slice_reduce_fusion
  9.5 0.6 and_select_fusion.first
  10.1 1.5 %convert_element_type.9 = bf16[2,64,64]{2,1,0:T(8,128)(2,1)} convert(s32[2,64,64]{2,1,0:T(8,128)} %param.15) | non-fusion elementwise | flops 8192 | bytes 49152 | tf_op jit(solution)/shard_map/convert_element_type | solution.py:512
  11.5 31.2 %exchange_in.1 = (bf16[2,8,256,128]{3,2,1,0:T(8,128)(2,1)}, bf16[2,2,512,256]{3,2,1,0:T(8,128)(2,1)}, bf16[2,2,512,256]{3,2,1,0:T(8,128)(2,1)}, f32[2,2,16,128]{3,2,1,0:T(8,128)}, bf16[2,128,64]{2,1,0:T(8,128)(2,1)}) custom-call(bf16[32,1024]{1,0:T(8,128)(2,1)} %keys.1, bf16[32,1024]{1,0:T(8,128)(2,1)} %values.1, bf16[512,256]{1,0:T(8,128)(2,1)} %queries.1, ...), custom_call_target="tpu_custom_call" | custom-call | tf_op jit(solution)/shard_map/exchange_in/pallas_call | solution.py:208
  42.7 0.0 copy-done
  42.8 20.0 %attend.1 = (f32[2,2,512,256]{3,2,1,0:T(8,128)}, f32[2,2048,128]{2,1,0:T(8,128)}) custom-call(s32[2]{0:T(128)} %pad_add_fusion.where_ref, s32[64]{0:T(128)} %order.1, s32[64]{0:T(128)} %and_select_fusion.first, bf16[2,2048,128]{2,1,0:T(8,128)(2,1)} %bitcast.13, bf16[2,2,512,256]{3,2,1,0:T(8,128)(2,1)} %get-tuple-element.11.q_all, ...), custom_call_target="tpu_custom_call" | custom-call | tf_op jit(solution)/shard_map/attend/pallas_call | solution.py:325
  62.8 30.3 %exchange_out.1 = (f32[512,256]{1,0:T(8,128)}, f32[32,1024]{1,0:T(8,128)}, f32[32,1024]{1,0:T(8,128)}) custom-call(f32[2,2,512,256]{3,2,1,0:T(8,128)} %get-tuple-element.15.dq_part, f32[2,2048,128]{2,1,0:T(8,128)} %get-tuple-element.16.dkv), custom_call_target="tpu_custom_call" | custom-call | tf_op jit(solution)/shard_map/exchange_out/pallas_call | solution.py:465
  93.1 1.9 %copy.15 = f32[512,256]{1,0:T(8,128)} copy(f32[512,256]{1,0:T(8,128)} %get-tuple-element.27) | data formatting | bytes 1048576
  95.0 1.6 %copy.16 = f32[32,1024]{1,0:T(8,128)} copy(f32[32,1024]{1,0:T(8,128)} %get-tuple-element.28) | data formatting | bytes 262144
  96.6 1.6 %copy.17 = f32[32,1024]{1,0:T(8,128)} copy(f32[32,1024]{1,0:T(8,128)} %get-tuple-element.29) | data formatting | bytes 262144
Async XLA Ops:
  9.4 33.4 %copy-start = (s32[64,128]{1,0:T(8,128)}, s32[64,128]{1,0:T(8,128)S(1)}, u32[]{:S(2)}) copy-start(s32[64,128]{1,0:T(8,128)S(1)} %select_bitcast_fusion.start) | copy-start | bytes 98308

commit v2 on v1

--- a/solution.py
+++ b/solution.py
@@ -14,13 +14,19 @@
 NBLK = 64
 NZ = 8
 TILE = 32
-CHUNK_TILES = 4
+CHUNK_TILES = 8
 CHUNK = TILE * CHUNK_TILES
 KEYS = NBLK * TILE
+PADDED = NBLK + CHUNK_TILES
 PLANE_KEYS = KEYS // NZ
 ROWS = 512
 NEVER = 1e30
 SCALE = D ** (-0.5)
+LOG2E = 1.4426950408889634
+MIB = 1 << 20
+IN_VMEM = 12 * MIB
+ATTEND_VMEM = 24 * MIB
+OUT_VMEM = 16 * MIB
 BF16 = jnp.bfloat16
 F32 = jnp.float32
 
@@ -61,9 +67,9 @@
 
 
 def gather_kernel(
-    keys, values, queries, grads, outs, norms, layout,
-    kv_all, q_all, g_all, s_all, l_all,
-    stats, a_send, a_recv, z_send, z_recv, y_send, y_recv, d_send, d_recv, f_send, f_recv,
+    keys, values, queries, grads, outs, norms, layout, ids,
+    kv_all, q_all, g_all, s_all, l_all, below,
+    stats, lay, a_send, a_recv, z_send, z_recv, y_send, y_recv, d_send, d_recv, f_send, f_recv,
 ):
     s, h, z, c, x, y = place()
     pair = h + 1 - 2 * (y % 2)
@@ -111,7 +117,7 @@
     y_copies = [
         send(queries, q_all.at[c, hp], y_send.at[0], y_recv.at[0], s, pair),
         send(grads, g_all.at[c, hp], y_send.at[1], y_recv.at[1], s, pair),
-        send(layout, l_all.at[hp], y_send.at[2], y_recv.at[2], s, pair),
+        send(lay, l_all.at[hp], y_send.at[2], y_recv.at[2], s, pair),
         send(stats, s_all.at[c, hp], y_send.at[3], y_recv.at[3], s, pair),
     ]
     d_copies = [
@@ -124,8 +130,9 @@
 
     ones = jnp.ones((8, D), BF16)
     for hh in range(2):
-        stats[hh * 4 : hh * 4 + 4, :] = norms[hh * 4 : hh * 4 + 4, :]
+        lay[hh * NBLK : (hh + 1) * NBLK, :] = layout[hh].astype(F32).astype(BF16)
         for rb in range(4):
+            stats[hh * 4 + rb : hh * 4 + rb + 1, :] = norms[hh : hh + 1, rb * BLOCK : (rb + 1) * BLOCK]
             at = (slice(rb * BLOCK, (rb + 1) * BLOCK), slice(hh * D, (hh + 1) * D))
             product = grads[at].astype(F32) * outs[at].astype(F32)
             high = product.astype(BF16)
@@ -137,9 +144,12 @@
     for copy in (y_copies[2], y_copies[3], d_copies[2]):
         copy.start()
     s_all[c, hp] = stats[...]
-    l_all[hp] = layout[...]
+    l_all[hp] = lay[...]
     q_all[c, hp] = queries[...]
     g_all[c, hp] = grads[...]
+    below[0] = 0
+    for d in range(1, 8):
+        below[d] = jnp.sum((ids[...] < d).astype(F32)).astype(jnp.int32)
 
     def piece(t, half, plane):
         return kv_all.at[t, plane, pl.ds(half * HALF, HALF), :]
@@ -202,7 +212,7 @@
         copy.wait_send()
 
 
-def gather(keys, values, queries, grads, outs, norms, layout):
+def gather(keys, values, queries, grads, outs, norms, layout, ids):
     vmem = pl.BlockSpec(memory_space=pltpu.VMEM)
     dma = pltpu.SemaphoreType.DMA
     return pl.pallas_call(
@@ -214,27 +224,34 @@
             jax.ShapeDtypeStruct((2, 2, ROWS, 2 * D), BF16),
             jax.ShapeDtypeStruct((2, 2, 16, BLOCK), F32),
             jax.ShapeDtypeStruct((2, 2 * NBLK, NBLK), BF16),
+            jax.ShapeDtypeStruct((8,), jnp.int32),
         ),
-        in_specs=[vmem] * 7,
-        out_specs=(vmem,) * 5,
+        in_specs=[vmem] * 8,
+        out_specs=(vmem,) * 5 + (pl.BlockSpec(memory_space=pltpu.SMEM),),
         scratch_shapes=[
             pltpu.VMEM((16, BLOCK), F32),
+            pltpu.VMEM((2 * NBLK, NBLK), BF16),
             dma((2, 8)), dma((2, 8)),
             dma((2, 4, 4)), dma((2, 4, 4)),
             dma((4,)), dma((4,)),
             dma((3,)), dma((3,)),
             dma((3,)), dma((3,)),
         ],
-        compiler_params=pltpu.CompilerParams(collective_id=0, has_side_effects=True),
-    )(keys, values, queries, grads, outs, norms, layout)
+        compiler_params=pltpu.CompilerParams(collective_id=0, has_side_effects=True, vmem_limit_bytes=IN_VMEM),
+    )(keys, values, queries, grads, outs, norms, layout, ids)
 
 
 def attend_kernel(
-    where_ref, order, first, kv, q_all, g_all, s_all, l_all, start,
+    order, below, kv, q_all, g_all, s_all, l_all,
     dq, dkv,
     ks, vs, dks, dvs, lay, pick, bias, qs, gs, dqt,
 ):
-    z, quarter = where_ref[0], where_ref[1]
+    _, _, z, c, _, y = place()
+    quarter = (y % 2) * 2 + c
+    edge = pl.ds(KEYS, CHUNK)
+    ks[edge, :] = jnp.zeros((CHUNK, D), BF16)
+    vs[edge, :] = jnp.zeros((CHUNK, D), BF16)
+    bias[NBLK:, :] = jnp.full((CHUNK_TILES, GROUP * BLOCK), NEVER, F32)
 
     def sort(sb, _):
         to = pl.ds(pl.multiple_of(order[sb] * TILE, TILE), TILE)
@@ -272,24 +289,29 @@
         norm = jnp.concatenate(norm, axis=1)
         delta = jnp.concatenate(delta, axis=1)
         seen = lax.dot_general(pick[...], spread, tn, preferred_element_type=F32)
-        bias[...] = jnp.where(seen > 0.5, norm, NEVER)
-        begin = start[pl.ds(block, 1), :]
-        begin = jnp.concatenate([begin] * GROUP, axis=1)
+        bias[:NBLK, :] = jnp.where(seen > 0.5, norm * LOG2E, NEVER)
         last = block * BLOCK + lax.broadcasted_iota(jnp.int32, (1, GROUP * BLOCK), 1) % BLOCK
+        begin = jnp.zeros_like(last)
+        first = 0
+        for d in range(1, 8):
+            begin = jnp.where(last >= below[d], below[d], begin)
+            first = jnp.where(block * BLOCK >= below[d], below[d], first)
+        first = first // BLOCK
         dqt[...] = jnp.zeros_like(dqt)
 
         def one_chunk(ch, _):
-            at = pl.ds(pl.multiple_of(ch * CHUNK, CHUNK), CHUNK)
+            tile0 = first + ch * CHUNK_TILES
+            at = pl.ds(pl.multiple_of(tile0 * TILE, TILE), CHUNK)
             kc, vc = ks[at, :], vs[at, :]
             scores = lax.dot_general(kc, qs[...], nt, preferred_element_type=F32)
             grad_scores = lax.dot_general(vc, gs[...], nt, preferred_element_type=F32)
             low, score_grad = [], []
             for t in range(CHUNK_TILES):
                 part = slice(t * TILE, (t + 1) * TILE)
-                tile = ch * CHUNK_TILES + t
+                tile = tile0 + t
                 position = row + (tile * BLOCK + quarter * TILE)
                 visible = (position >= begin) & (position <= last)
-                weights = jnp.exp(scores[part, :] * SCALE - bias[pl.ds(tile, 1), :])
+                weights = jnp.exp2(scores[part, :] * (SCALE * LOG2E) - bias[pl.ds(tile, 1), :])
                 weights = jnp.where(visible, weights, 0.0)
                 low.append(weights.astype(BF16))
                 score_grad.append((weights * (grad_scores[part, :] - delta)).astype(BF16))
@@ -300,7 +322,7 @@
             dqt[...] += lax.dot_general(kc, score_grad, tn, preferred_element_type=F32)
             return 0
 
-        lax.fori_loop(first[block] // CHUNK_TILES, block // CHUNK_TILES + 1, one_chunk, 0)
+        lax.fori_loop(0, (block - first) // CHUNK_TILES + 1, one_chunk, 0)
         for head in range(GROUP):
             hp, hh = head // 2, head % 2
             block_grad = dqt[:, head * BLOCK : (head + 1) * BLOCK].T
@@ -319,7 +341,7 @@
     lax.fori_loop(0, NBLK, unsort, 0, unroll=8)
 
 
-def attend(where, order, first, kv, q_all, g_all, s_all, l_all, start):
+def attend(order, below, kv, q_all, g_all, s_all, l_all):
     vmem = pl.BlockSpec(memory_space=pltpu.VMEM)
     smem = pl.BlockSpec(memory_space=pltpu.SMEM)
     return pl.pallas_call(
@@ -329,27 +351,28 @@
             jax.ShapeDtypeStruct((2, 2, ROWS, 2 * D), F32),
             jax.ShapeDtypeStruct((2, KEYS, D), F32),
         ),
-        in_specs=[smem] * 3 + [vmem] * 6,
+        in_specs=[smem] * 2 + [vmem] * 5,
         out_specs=(vmem, vmem),
         scratch_shapes=[
-            pltpu.VMEM((KEYS, D), BF16),
-            pltpu.VMEM((KEYS, D), BF16),
-            pltpu.VMEM((KEYS, D), F32),
-            pltpu.VMEM((KEYS, D), F32),
+            pltpu.VMEM((PADDED * TILE, D), BF16),
+            pltpu.VMEM((PADDED * TILE, D), BF16),
+            pltpu.VMEM((PADDED * TILE, D), F32),
+            pltpu.VMEM((PADDED * TILE, D), F32),
             pltpu.VMEM((GROUP * NBLK, NBLK), F32),
             pltpu.VMEM((8, NBLK), F32),
-            pltpu.VMEM((NBLK, GROUP * BLOCK), F32),
+            pltpu.VMEM((PADDED, GROUP * BLOCK), F32),
             pltpu.VMEM((GROUP * BLOCK, D), BF16),
             pltpu.VMEM((GROUP * BLOCK, D), BF16),
             pltpu.VMEM((D, GROUP * BLOCK), F32),
         ],
-    )(where, order, first, kv, q_all, g_all, s_all, l_all, start)
+        compiler_params=pltpu.CompilerParams(vmem_limit_bytes=ATTEND_VMEM),
+    )(order, below, kv, q_all, g_all, s_all, l_all)
 
 
 def scatter_kernel(
     dq_part, dkv,
-    dq, dk, dv,
-    twin_in, pair_out, pair_in, z_out, z_in, fin, own_in,
+    dq, pair_in, own_in,
+    twin_in, pair_out, z_out, z_in, fin,
     d_send, d_recv, y_send, y_recv, z_send, z_recv, a_send, a_recv,
 ):
     s, h, z, c, x, y = place()
@@ -445,13 +468,9 @@
                 own_in[g] = fin[half * 4 + k]
 
     y_copy.wait_recv()
-    dq[...] += pair_in[...].astype(F32)
-
     for g, (seq, head, other) in enumerate(makers):
         landed = send(fin.at[0], own_in.at[g], a_send.at[0], a_recv.at[g], seq, head)
         pl.when(other)(landed.wait_recv)
-        dk[:, g * D : (g + 1) * D] = own_in[g, 0]
-        dv[:, g * D : (g + 1) * D] = own_in[g, 1]
 
     for copy, other in a_copies:
         pl.when(other)(copy.wait_send)
@@ -467,54 +486,66 @@
         name="exchange_out",
         out_shape=(
             jax.ShapeDtypeStruct((ROWS, 2 * D), F32),
-            jax.ShapeDtypeStruct((TILE, 8 * D), F32),
-            jax.ShapeDtypeStruct((TILE, 8 * D), F32),
+            jax.ShapeDtypeStruct((ROWS, 2 * D), BF16),
+            jax.ShapeDtypeStruct((8, 2, TILE, D), F32),
         ),
         in_specs=[vmem] * 2,
         out_specs=(vmem,) * 3,
         scratch_shapes=[
             pltpu.VMEM((2, ROWS, 2 * D), F32),
             pltpu.VMEM((ROWS, 2 * D), BF16),
-            pltpu.VMEM((ROWS, 2 * D), BF16),
             pltpu.VMEM((2, 4, 4, HALF, D), BF16),
             pltpu.VMEM((2, 4, 4, HALF, D), BF16),
-            pltpu.VMEM((8, 2, TILE, D), F32),
             pltpu.VMEM((8, 2, TILE, D), F32),
             dma((1,)), dma((1,)),
             dma((1,)), dma((1,)),
             dma((2, 4, 4)), dma((2, 4, 4)),
             dma((8,)), dma((8,)),
         ],
-        compiler_params=pltpu.CompilerParams(collective_id=1, has_side_effects=True),
+        compiler_params=pltpu.CompilerParams(collective_id=1, has_side_effects=True, vmem_limit_bytes=OUT_VMEM),
     )(dq_part, dkv)
+
+
+def finish_kernel(sums, pair_in, own_in, dq, dk, dv):
+    dq[...] = sums[...] + pair_in[...].astype(F32)
+    for g in range(8):
+        dk[:, g * D : (g + 1) * D] = own_in[g, 0]
+        dv[:, g * D : (g + 1) * D] = own_in[g, 1]
+
+
+def finish(sums, pair_in, own_in):
+    vmem = pl.BlockSpec(memory_space=pltpu.VMEM)
+    return pl.pallas_call(
+        finish_kernel,
+        name="finish",
+        out_shape=(
+            jax.ShapeDtypeStruct((ROWS, 2 * D), F32),
+            jax.ShapeDtypeStruct((TILE, 8 * D), F32),
+            jax.ShapeDtypeStruct((TILE, 8 * D), F32),
+        ),
+        in_specs=[vmem] * 3,
+        out_specs=(vmem,) * 3,
+        compiler_params=pltpu.CompilerParams(vmem_limit_bytes=8 * MIB),
+    )(sums, pair_in, own_in)
 
 
 def body(
     queries, keys, values, attn_out, out_grad, log_norm, block_layout, document_ids, block_order
 ):
-    _, _, z, c, _, y = place()
-    where = jnp.stack([z, (y % 2) * 2 + c]).astype(jnp.int32)
-    below = jnp.sum(
-        (document_ids[None, :] < jnp.arange(8, dtype=jnp.int32)[:, None]).astype(jnp.int32), axis=1
-    )
-    ids = document_ids.reshape(NBLK, BLOCK)
-    start = jnp.zeros_like(ids)
-    for d in range(1, 8):
-        start = jnp.where(ids == d, below[d], start)
-    first = start[:, 0] // BLOCK
-    kv, q_all, g_all, s_all, l_all = gather(
+    kv, q_all, g_all, s_all, l_all, below = gather(
         keys,
         values,
         queries,
         out_grad,
         attn_out,
-        log_norm.reshape(8, BLOCK),
-        block_layout.reshape(2 * NBLK, NBLK).astype(BF16),
+        log_norm,
+        block_layout,
+        document_ids.reshape(NBLK, BLOCK),
     )
     dq_part, dkv = attend(
-        where, block_order, first, kv.reshape(2, KEYS, D), q_all, g_all, s_all, l_all, start
+        block_order, below, kv.reshape(2, KEYS, D), q_all, g_all, s_all, l_all
     )
-    return scatter(dq_part, dkv)
+    return finish(*scatter(dq_part, dkv))
 
 
 def solution(mesh):

time: 99 us -> 80.8 us (0.82)
  Pallas kernels: 81.6 us -> 72.4 us
  other arithmetic: 8.77 us -> 0 us
    pallas_call x1, Pallas kernels: 20 us -> 13.8 us  [attend(): pl.pallas_call(attend_kernel, name='attend', out_shape=(jax.ShapeDtypeStr...]
    select_n x2 -> x0, other arithmetic: 5.77 us -> none  [the longest x1 5.19 us: body(): start = jnp.where(ids == d, below[d], start)]
    unnamed x5 -> x18, local copies, waits for them, and re-layouts: 5.01 us -> 7.45 us
    pallas_call x1, Pallas kernels: 31.2 us -> 28.9 us  [gather(): pl.pallas_call(gather_kernel, name='exchange_in', out_shape=(jax.ShapeDty...]
    pallas_call x1, Pallas kernels: 30.3 us -> 28.8 us  [scatter(): pl.pallas_call(scatter_kernel, name='exchange_out', out_shape=(jax.ShapeD...]
    convert_element_type x1 -> x0, other arithmetic: 1.46 us -> none  [body(): block_layout.reshape(2 * NBLK, NBLK).astype(BF16)]
    reshape x1 -> x0, local copies, waits for them, and re-layouts: 1.29 us -> none  [body(): log_norm.reshape(8, BLOCK)]
where the time goes in v2:
time: 80.8 us; the launch traced here: 80.6 us
  Pallas kernels  72.4 us (90%)
  local copies, waits for them, and re-layouts  7.45 us (9%)
    pallas_call x1, Pallas kernels, gather(): pl.pallas_call(gather_kernel, name='exchange_in', out_shape=(jax.ShapeDty...  28.9 us
    pallas_call x1, Pallas kernels, scatter(): pl.pallas_call(scatter_kernel, name='exchange_out', out_shape=(jax.ShapeD...  28.8 us
    pallas_call x1, Pallas kernels, attend(): pl.pallas_call(attend_kernel, name='attend', out_shape=(jax.ShapeDtypeStr...  13.8 us
    unnamed x18, local copies, waits for them, and re-layouts  7.45 us

profile of v2, /device:TPU:1, one launch (start us, length us, event | category | flops | bytes accessed | tf_op | source)
XLA Modules:
  0.0 80.6 jit_solution(2159347388187640647)
XLA Ops:
  0.6 0.0 copy-start
  0.6 0.9 %copy-done = bf16[512,256]{1,0:T(8,128)(2,1)S(1)} copy-done((bf16[512,256]{1,0:T(8,128)(2,1)S(1)}, bf16[512,256]{1,0:T(8,128)(2,1)}, u32[]{:S(2)}) %copy-start) | copy-done | bytes 262168
  1.6 0.0 copy-start.1
  1.6 0.9 %copy-done.1 = bf16[512,256]{1,0:T(8,128)(2,1)S(1)} copy-done((bf16[512,256]{1,0:T(8,128)(2,1)S(1)}, bf16[512,256]{1,0:T(8,128)(2,1)}, u32[]{:S(2)}) %copy-start.1) | copy-done | bytes 262168
  2.5 0.0 copy-start.2
  2.5 0.9 %copy-done.2 = bf16[512,256]{1,0:T(8,128)(2,1)S(1)} copy-done((bf16[512,256]{1,0:T(8,128)(2,1)S(1)}, bf16[512,256]{1,0:T(8,128)(2,1)}, u32[]{:S(2)}) %copy-start.2) | copy-done | bytes 262168
  3.5 0.0 copy-start.3
  3.5 0.8 %copy-done.3 = bf16[32,1024]{1,0:T(8,128)(2,1)S(1)} copy-done((bf16[32,1024]{1,0:T(8,128)(2,1)S(1)}, bf16[32,1024]{1,0:T(8,128)(2,1)}, u32[]{:S(2)}) %copy-start.3) | copy-done | bytes 65560
  4.3 0.0 copy-start.4
  4.3 0.8 %copy-done.4 = bf16[32,1024]{1,0:T(8,128)(2,1)S(1)} copy-done((bf16[32,1024]{1,0:T(8,128)(2,1)S(1)}, bf16[32,1024]{1,0:T(8,128)(2,1)}, u32[]{:S(2)}) %copy-start.4) | copy-done | bytes 65560
  5.2 0.0 copy-start.5
  5.2 0.8 %copy-done.5 = s32[2,64,64]{2,1,0:T(8,128)S(1)} copy-done((s32[2,64,64]{2,1,0:T(8,128)S(1)}, s32[2,64,64]{2,1,0:T(8,128)}, u32[]{:S(2)}) %copy-start.5) | copy-done | bytes 32792
  6.0 0.0 copy-start.6
  6.0 0.8 copy-done.6
  6.8 0.0 copy-start.7
  6.8 0.7 copy-done.7
  7.5 28.9 %exchange_in.1 = (bf16[2,8,256,128]{3,2,1,0:T(8,128)(2,1)S(1)}, bf16[2,2,512,256]{3,2,1,0:T(8,128)(2,1)S(1)}, bf16[2,2,512,256]{3,2,1,0:T(8,128)(2,1)S(1)}, f32[...) custom-call(bf16[32,1024]{1,0:T(8,128)(2,1)S(1)} %copy-done.3, ...), custom_call_target="tpu_custom_call" | custom-call | tf_op jit(solution)/shard_map/exchange_in/pallas_call | solution.py:218
  36.4 0.0 copy-start.8
  36.4 0.6 copy-done.8
  37.0 13.8 %attend.1 = (f32[2,2,512,256]{3,2,1,0:T(8,128)S(1)}, f32[2,2048,128]{2,1,0:T(8,128)S(1)}) custom-call(s32[64]{0:T(128)S(1)} %copy-done.8, s32[8]{0:T(128)S(1)} %get-tuple-element.14.below, bf16[2,2048,128]{2,1,0:T(8,128)(2,1)S(1)} %bitcast.2, bf16[2,2,512,256]{3,2,1,0:T(8,128)(2,1)S(1)} %get-tuple-element.16.q_all, ...), custom_call_target="tpu_custom_call" | custom-call | tf_op jit(solution)/shard_map/attend/pallas_call | solution.py:347
  50.8 28.8 %exchange_out.1 = (f32[512,256]{1,0:T(8,128)S(1)}, bf16[512,256]{1,0:T(8,128)(2,1)S(1)}, f32[8,2,32,128]{3,2,1,0:T(8,128)S(1)}) custom-call(f32[2,2,512,256]{3,2,1,0:T(8,128)S(1)} %get-tuple-element.20.dq_part, f32[2,2048,128]{2,1,0:T(8,128)S(1)} %get-tuple-element.21.dkv), custom_call_target="tpu_custom_call" | custom-call | tf_op jit(solution)/shard_map/exchange_out/pallas_call | solution.py:484
  79.6 0.9 %finish.1 = (f32[512,256]{1,0:T(8,128)}, f32[32,1024]{1,0:T(8,128)}, f32[32,1024]{1,0:T(8,128)}) custom-call(f32[512,256]{1,0:T(8,128)S(1)} %get-tuple-element.22.sums, bf16[512,256]{1,0:T(8,128)(2,1)S(1)} %get-tuple-element.23.pair_in, f32[8,2,32,128]{3,2,1,0:T(8,128)S(1)} %get-tuple-element.24.own_in), custom_call_target="tpu_custom_call" | custom-call | tf_op jit(solution)/shard_map/finish/pallas_call | solution.py:518
Async XLA Ops:
  0.6 1.0 %copy-start = (bf16[512,256]{1,0:T(8,128)(2,1)S(1)}, bf16[512,256]{1,0:T(8,128)(2,1)}, u32[]{:S(2)}) copy-start(bf16[512,256]{1,0:T(8,128)(2,1)} %queries.1) | copy-start | bytes 786436
  1.6 0.9 %copy-start.1 = (bf16[512,256]{1,0:T(8,128)(2,1)S(1)}, bf16[512,256]{1,0:T(8,128)(2,1)}, u32[]{:S(2)}) copy-start(bf16[512,256]{1,0:T(8,128)(2,1)} %grads.1) | copy-start | bytes 786436
  2.5 0.9 %copy-start.2 = (bf16[512,256]{1,0:T(8,128)(2,1)S(1)}, bf16[512,256]{1,0:T(8,128)(2,1)}, u32[]{:S(2)}) copy-start(bf16[512,256]{1,0:T(8,128)(2,1)} %outs.1) | copy-start | bytes 786436
  3.5 0.8 %copy-start.3 = (bf16[32,1024]{1,0:T(8,128)(2,1)S(1)}, bf16[32,1024]{1,0:T(8,128)(2,1)}, u32[]{:S(2)}) copy-start(bf16[32,1024]{1,0:T(8,128)(2,1)} %keys.1) | copy-start | bytes 196612
  4.3 0.8 %copy-start.4 = (bf16[32,1024]{1,0:T(8,128)(2,1)S(1)}, bf16[32,1024]{1,0:T(8,128)(2,1)}, u32[]{:S(2)}) copy-start(bf16[32,1024]{1,0:T(8,128)(2,1)} %values.1) | copy-start | bytes 196612
  5.2 0.8 %copy-start.5 = (s32[2,64,64]{2,1,0:T(8,128)S(1)}, s32[2,64,64]{2,1,0:T(8,128)}, u32[]{:S(2)}) copy-start(s32[2,64,64]{2,1,0:T(8,128)} %layout.1) | copy-start | bytes 98308
  6.0 0.8 copy-start.6
  6.8 0.7 copy-start.7
  36.4 0.7 copy-start.8

commit v3 on v0

v3 whole, which is shorter than its diff:
```python
import jax
import jax.numpy as jnp
from jax import lax
from jax.experimental import pallas as pl
from jax.experimental.pallas import tpu as pltpu
from jax.sharding import PartitionSpec as P

MESH = pl.DeviceIdType.MESH
D = 128
BLOCK = 128
NBLK = 64
NZ = 8
TILE = 32
TILES = 8
PLANE = TILE * TILES
HALF = PLANE // 2
ROWS = 512
COLS = 512
BIG = 1e30
ALWAYS = 1 << 20
SCALE = D ** (-0.5)
LOG2E = 1.4426950408889634
BF16 = jnp.bfloat16
F32 = jnp.float32
NN = (((1,), (0,)), ((), ()))
NT = (((1,), (1,)), ((), ()))
TN = (((0,), (0,)), ((), ()))
AT_DOC = 64
AT_ONE = 72
SUBS = ((0, 0), (0, 1), (1, 0), (1, 1))
MIB = 1 << 20


def place():
    s = lax.axis_index("seq")
    h = lax.axis_index("head")
    return s, h, s // 2, s % 2, h // 4, h % 4


def send(src, dst, send_sem, recv_sem, seq, head):
    return pltpu.make_async_remote_copy(
        src_ref=src,
        dst_ref=dst,
        send_sem=send_sem,
        recv_sem=recv_sem,
        device_id=(seq, head),
        device_id_type=MESH,
    )


def dot(a, b, dims):
    return lax.dot_general(a, b, dims, preferred_element_type=F32)


def three(x):
    high = x.astype(BF16)
    rest = x - high.astype(F32)
    mid = rest.astype(BF16)
    low = (rest - mid.astype(F32)).astype(BF16)
    return [high, mid, low]


def iota(shape, dim):
    return lax.broadcasted_iota(jnp.int32, shape, dim)


def fused_kernel(
    keys_h, values_h, queries_h, grads_h, outs_h, norms_h, layout_h, ids_h, order_h, order,
    dq, pair_in, own_in,
    keys, values, queries, grads, outs, norms, layout, ids, order_v,
    kv, q_in, g_in, stats, s_in, lay, l_in, lperm, span,
    ax, qu, gu, qx, gx, acc, dqt, dqp, twin_in, pair_out, z_out, z_in, fin, ahead,
    l_sem, a_send, a_recv, k_send, k_recv, z_send, z_recv, y_send, y_recv, d_send, d_recv,
    f_send, f_recv, r_send, r_recv, b_send, b_recv,
):
    s, h, z, c, x, y = place()
    pair = h + 1 - 2 * (y % 2)
    twin = s + 1 - 2 * c
    up = ((z + 1) % NZ) * 2 + c
    down = ((z + NZ - 1) % NZ) * 2 + c
    hp = y % 2
    quarter = hp * 2 + c

    loads = []
    for i, (src, dst) in enumerate((
        (keys_h, keys), (values_h, values), (queries_h, queries), (grads_h, grads), (outs_h, outs),
        (norms_h, norms), (layout_h, layout), (ids_h, ids), (order_h, order_v),
    )):
        loads.append(pltpu.make_async_copy(src, dst, l_sem.at[i]))
        loads[i].start()

    takers, givers = [], []
    for xg in range(4):
        for yp in range(2):
            seq, head = z * 2 + y % 2, xg * 4 + yp * 2 + y // 2
            takers.append((seq, head, (seq != s) | (head != h)))
    for cg in range(2):
        for xg in range(4):
            seq, head = z * 2 + cg, xg * 4 + quarter
            givers.append((seq, head, (seq != s) | (head != h)))
    barrier = pltpu.get_barrier_semaphore()
    for seq, head in ((s, pair), (twin, h), (up, h), (down, h)):
        pl.semaphore_signal(barrier, inc=1, device_id=(seq, head), device_id_type=MESH)
    for seq, head, other in takers + givers:

        @pl.when(other)
        def _():
            pl.semaphore_signal(barrier, inc=1, device_id=(seq, head), device_id_type=MESH)

    own = ((y % 2 == c) & (y // 2 == hp)).astype(jnp.int32)
    acc[...] = jnp.zeros_like(acc)
    dqt[...] = jnp.zeros_like(dqt)
    for load in loads[:3]:
        load.wait()
    pl.semaphore_wait(barrier, 4 + 16 - 2 * own)

    slot = c * 4 + x
    slot_rows = pl.ds(pl.multiple_of(slot * TILE, TILE), TILE)
    a_copies = []
    for g, (seq, head, other) in enumerate(takers):
        for t, src in enumerate((keys, values)):
            copy = send(
                src.at[:, pl.ds(g * D, D)], kv.at[t, z, slot_rows, :],
                a_send.at[t, g], a_recv.at[t, slot], seq, head,
            )
            pl.when(other)(copy.start)
            a_copies.append((copy, other))

            @pl.when(jnp.logical_not(other))
            def _():
                kv[t, z, slot_rows, :] = src[:, g * D : (g + 1) * D]

    y_copies = [
        send(queries, q_in.at[1], y_send.at[0], y_recv.at[0], s, pair),
        send(grads, g_in.at[1], y_send.at[1], y_recv.at[1], s, pair),
        send(lay, l_in, y_send.at[2], y_recv.at[2], s, pair),
        send(stats, s_in.at[1], y_send.at[3], y_recv.at[3], s, pair),
    ]
    d_copies = [
        send(queries, q_in.at[0], d_send.at[0], d_recv.at[0], twin, h),
        send(grads, g_in.at[0], d_send.at[1], d_recv.at[1], twin, h),
        send(stats, s_in.at[0], d_send.at[2], d_recv.at[2], twin, h),
    ]
    y_copies[0].start()
    d_copies[0].start()
    for load in loads[3:]:
        load.wait()
    y_copies[1].start()
    d_copies[1].start()

    ones = jnp.ones((8, D), BF16)
    for hh in range(2):
        lay[hh * NBLK : (hh + 1) * NBLK, :] = layout[hh].astype(F32).astype(BF16)
        for rb in range(4):
            at = (slice(rb * BLOCK, (rb + 1) * BLOCK), slice(hh * D, (hh + 1) * D))
            product = grads[at].astype(F32) * outs[at].astype(F32)
            high = product.astype(BF16)
            low = (product - high.astype(F32)).astype(BF16)
            total = dot(ones, high, NT) + dot(ones, low, NT)
            stats[hh * 4 + rb : hh * 4 + rb + 1, :] = norms[hh : hh + 1, rb * BLOCK : (rb + 1) * BLOCK]
            stats[8 + hh * 4 + rb : 9 + hh * 4 + rb, :] = total[0:1, :]
    for copy in (y_copies[2], y_copies[3], d_copies[2]):
        copy.start()

    lane = iota((1, D), 1)
    first, after = jnp.zeros((1, D), F32), jnp.full((1, D), float(ALWAYS), F32)
    for d in range(1, 8):
        below = jnp.sum((ids[...] < d).astype(F32), axis=(0, 1), keepdims=True)
        first = jnp.where(lane == AT_DOC + d, below, first)
        after = jnp.where(lane == AT_DOC + d - 1, below, after)
    span[0:1, :] = first.astype(jnp.int32)
    span[1:2, :] = after.astype(jnp.int32)

    stored = (iota((NBLK, D), 0) == order_v[...]) & (iota((NBLK, D), 1) < NBLK)
    stored = stored.astype(F32).astype(BF16)
    lperm[0] = dot(lay[...], stored, NN)

    ahead[...] = quarter * TILE + iota((TILE, COLS), 0) - iota((TILE, COLS), 1) % BLOCK
    extra = (iota((8, D), 1) - AT_ONE == iota((8, D), 0)) & (iota((8, D), 0) < 3)
    extra = extra.astype(F32).astype(BF16)
    tile_lane = iota((1, D), 1) < NBLK
    doc_lane = (lane >= AT_DOC) & (lane < AT_ONE)

    def prepare(side, cb, q_piece, g_piece, s_piece):
        for rp in range(2):
            unit = cb * 2 + rp
            norm, delta = [], []
            for b in range(2):
                rb = rp * 2 + b
                for hh in range(2):
                    rows = pl.ds((b * 2 + hh) * BLOCK, BLOCK)
                    at = (slice(rb * BLOCK, (rb + 1) * BLOCK), slice(hh * D, (hh + 1) * D))
                    qu[side, unit, rows, :] = q_piece[at]
                    gu[side, unit, rows, :] = g_piece[at]
                    norm.append(s_piece[hh * 4 + rb : hh * 4 + rb + 1, :])
                    delta.append(s_piece[8 + hh * 4 + rb : 9 + hh * 4 + rb, :])
            zero = jnp.zeros((5, COLS), BF16)
            norm = jnp.concatenate(norm, axis=1) * (-1.0 / SCALE)
            delta = -jnp.concatenate(delta, axis=1)
            norm = dot(jnp.concatenate(three(norm) + [zero], axis=0), extra, TN)
            delta = dot(jnp.concatenate(three(delta) + [zero], axis=0), extra, TN)
            gx[side, unit] = delta.astype(BF16)
            for b in range(2):
                block = order[z * 8 + unit * 2 + b]
                position = block * BLOCK + iota((BLOCK, D), 0)
                apart = doc_lane & ((position < span[0:1, :]) | (position >= span[1:2, :]))
                for hh in range(2):
                    rows = pl.ds((b * 2 + hh) * BLOCK, BLOCK)
                    seen = lperm[side, pl.ds(hh * NBLK + block, 1), :]
                    hidden = tile_lane & ((seen < 0.5) | (order_v[...] > block))
                    base = norm[(b * 2 + hh) * BLOCK : (b * 2 + hh + 1) * BLOCK, :]
                    qx[side, unit, rows, :] = jnp.where(apart | hidden, -BIG, base).astype(BF16)

    def prepare_keys(plane):
        row, col = iota((TILE, D), 0), iota((TILE, D), 1)
        for t in range(TILES):
            position = order[plane * TILES + t] * BLOCK + quarter * TILE + row
            hot = col == plane * TILES + t
            hot = hot | (doc_lane & (position >= span[0:1, :]) & (position < span[1:2, :]))
            hot = hot | ((col >= AT_ONE) & (col < AT_ONE + 3))
            ax[plane, pl.ds(t * TILE, TILE), :] = hot.astype(F32).astype(BF16)

    def unit_grads(side, plane, unit):
        kc, vc, extra_k = kv[0, plane], kv[1, plane], ax[plane]
        q, g = qu[side, unit], gu[side, unit]
        scores = dot(jnp.concatenate([kc, extra_k], 1), jnp.concatenate([q, qx[side, unit]], 1), NT)
        grads_less = dot(jnp.concatenate([vc, extra_k], 1), jnp.concatenate([g, gx[side, unit]], 1), NT)
        low, score_grad = [], []
        for t in range(TILES):
            part = slice(t * TILE, (t + 1) * TILE)
            bound = []
            for b in range(2):
                same = order[plane * TILES + t] == order[z * 8 + unit * 2 + b]
                bound.append(jnp.full((1, 2 * BLOCK), jnp.where(same, 0, ALWAYS), jnp.int32))
            visible = ahead[...] <= jnp.concatenate(bound, axis=1)
            weights = jnp.where(visible, jnp.exp2(scores[part, :] * (SCALE * LOG2E)), 0.0)
            low.append(weights.astype(BF16))
            score_grad.append((weights * grads_less[part, :]).astype(BF16))
        low = jnp.concatenate(low, axis=0)
        score_grad = jnp.concatenate(score_grad, axis=0)
        acc[0, plane] += dot(score_grad, q, NN)
        acc[1, plane] += dot(low, g, NN)
        dqt[side, unit] += dot(kc, score_grad, TN)

    def compute(side, plane, units=(0, 4)):
        def one(unit, _):
            unit_grads(side, plane, unit)
            return 0

        lax.fori_loop(units[0], units[1], one, 0)

    def query_sums(side, cb):
        for rp in range(2):
            for b in range(2):
                for hh in range(2):
                    at = b * 2 + hh
                    block_grad = dqt[side, cb * 2 + rp, :, at * BLOCK : (at + 1) * BLOCK].T * SCALE
                    dqp[side, cb, (rp * 2 + b) * BLOCK : (rp * 2 + b + 1) * BLOCK, hh * D : (hh + 1) * D] = block_grad

    def hop_in(way, step, sub):
        t, half = SUBS[sub]
        origin = (z + NZ - (step - 1)) % NZ if way == 0 else (z + step - 1) % NZ
        piece = kv.at[t, origin, pl.ds(half * HALF, HALF), :]
        return send(
            piece, piece, k_send.at[way, step - 1, sub], k_recv.at[way, step - 1, sub],
            up if way == 0 else down, h,
        )

    def carries(way, step, sub):
        return step < 4 or (step == 4 and SUBS[sub][0] == way)

    k_copies = {}
    for sub, (t, half) in enumerate(SUBS):
        for k in range(4):
            at = half * 4 + k
            seq, head, other = givers[at]
            landed = send(
                keys.at[:, pl.ds(0, D)], kv.at[t, z, pl.ds(at * TILE, TILE), :],
                a_send.at[t, 0], a_recv.at[t, at], seq, head,
            )
            pl.when(other)(landed.wait_recv)
        for way in range(2):
            k_copies[way, 1, sub] = hop_in(way, 1, sub)
            k_copies[way, 1, sub].start()

    forwards = []

    def pass_on(k, ref):
        y_copies[k].wait_recv()
        i = len(forwards)
        copy = send(ref.at[1], ref.at[2], f_send.at[i], f_recv.at[i], twin, h)
        copy.start()
        forwards.append(copy)

    def arrive(step):
        for sub in range(4):
            for way in range(2):
                if carries(way, step, sub):
                    k_copies[way, step, sub].wait_recv()
                if carries(way, step + 1, sub):
                    k_copies[way, step + 1, sub] = hop_in(way, step + 1, sub)
                    k_copies[way, step + 1, sub].start()

    prepare(0, c, queries, grads, stats)
    for copy in d_copies:
        copy.wait_recv()
    prepare(0, 1 - c, q_in.at[0], g_in.at[0], s_in.at[0])
    prepare_keys(z)
    above = [(z + d) % NZ for d in range(5)]
    under = [(z + NZ - d) % NZ for d in range(4)]

    compute(0, z)
    arrive(1)
    for plane in (above[1], under[1]):
        prepare_keys(plane)
        compute(0, plane)
        if plane is above[1]:
            arrive(2)
    pass_on(0, q_in)
    for plane in (above[2], under[2]):
        prepare_keys(plane)
        compute(0, plane)
        if plane is above[2]:
            arrive(3)
    pass_on(1, g_in)
    pass_on(3, s_in)
    y_copies[2].wait_recv()
    lperm[1] = dot(l_in[...], stored, NN)
    for plane in (above[3], under[3]):
        prepare_keys(plane)
        compute(0, plane)
        if plane is above[3]:
            arrive(4)
    prepare_keys(above[4])
    compute(0, above[4])
    query_sums(0, 1 - c)
    own_copies = [send(dqp.at[0, 1 - c], twin_in.at[0], r_send.at[0], r_recv.at[0], twin, h)]
    own_copies[0].start()
    prepare(1, c, q_in.at[1], g_in.at[1], s_in.at[1])
    for copy in forwards:
        copy.wait_recv()
    prepare(1, 1 - c, q_in.at[2], g_in.at[2], s_in.at[2])

    z_copies = {}

    def hop_out(way, step, sub):
        t, half = SUBS[sub]
        target = (z + 5 - step) % NZ if way == 0 else (z + NZ - (5 - step)) % NZ
        value = acc[t, target, half * HALF : (half + 1) * HALF, :]
        if (way, step - 1, sub) in z_copies:
            z_copies[way, step - 1, sub].wait_recv()
            value = value + z_in[way, step - 2, sub].astype(F32)
        z_out[way, step - 1, sub] = value.astype(BF16)
        copy = send(
            z_out.at[way, step - 1, sub], z_in.at[way, step - 1, sub],
            z_send.at[way, step - 1, sub], z_recv.at[way, step - 1, sub],
            up if way == 0 else down, h,
        )
        copy.start()
        z_copies[way, step, sub] = copy

    compute(1, above[4])
    for sub in range(4):
        hop_out(SUBS[sub][0], 1, sub)
    for d in (3, 2, 1):
        for way in range(2):
            compute(1, above[d] if way == 0 else under[d])
            for sub in (2, 3, 0, 1) if way == 0 else (0, 1, 2, 3):
                hop_out(way, 5 - d, sub)
    compute(1, z, ((1 - c) * 2, (1 - c) * 2 + 2))
    query_sums(1, 1 - c)
    own_copies.append(send(dqp.at[1, 1 - c], twin_in.at[1], r_send.at[1], r_recv.at[1], twin, h))
    own_copies[1].start()
    compute(1, z, (c * 2, c * 2 + 2))
    query_sums(1, c)
    own_copies[1].wait_recv()
    pair_out[...] = (dqp[1, c] + twin_in[1]).astype(BF16)
    own_copies.append(send(pair_out, pair_in, r_send.at[2], r_recv.at[2], s, pair))
    own_copies[2].start()

    b_copies = []
    g = x * 2 + y // 2
    for half in range(2):
        for t in range(2):
            sub = t * 2 + half
            value = acc[t, z, half * HALF : (half + 1) * HALF, :]
            for way in range(2):
                z_copies[way, 4, sub].wait_recv()
                value = value + z_in[way, 3, sub].astype(F32)
            if t == 0:
                value = value * SCALE
            for k in range(4):
                fin[half * 4 + k, t] = value[k * TILE : (k + 1) * TILE, :]
        for k in range(4):
            seq, head, other = givers[half * 4 + k]
            copy = send(
                fin.at[half * 4 + k], own_in.at[g], b_send.at[half * 4 + k], b_recv.at[g], seq, head,
            )
            pl.when(other)(copy.start)
            b_copies.append((copy, other))

            @pl.when(jnp.logical_not(other))
            def _():
                own_in[g] = fin[half * 4 + k]

    query_sums(0, c)
    own_copies[0].wait_recv()
    dq[...] = dqp[0, c] + twin_in[0]

    for g, (seq, head, other) in enumerate(takers):
        landed = send(fin.at[0], own_in.at[g], b_send.at[0], b_recv.at[g], seq, head)
        pl.when(other)(landed.wait_recv)
    own_copies[2].wait_recv()

    for copy, other in a_copies + b_copies:
        pl.when(other)(copy.wait_send)
    for copy in list(k_copies.values()) + list(z_copies.values()):
        copy.wait_send()
    for copy in y_copies + d_copies + forwards + own_copies:
        copy.wait_send()


def fused(keys, values, queries, grads, outs, norms, layout, ids, order):
    vmem = pl.BlockSpec(memory_space=pltpu.VMEM)
    smem = pl.BlockSpec(memory_space=pltpu.SMEM)
    hbm = pl.BlockSpec(memory_space=pltpu.HBM)
    dma = pltpu.SemaphoreType.DMA
    v = pltpu.VMEM
    return pl.pallas_call(
        fused_kernel,
        name="fused",
        out_shape=(
            jax.ShapeDtypeStruct((ROWS, 2 * D), F32),
            jax.ShapeDtypeStruct((ROWS, 2 * D), BF16),
            jax.ShapeDtypeStruct((8, 2, TILE, D), F32),
        ),
        in_specs=[hbm] * 9 + [smem],
        out_specs=(vmem,) * 3,
        scratch_shapes=[
            v((TILE, 8 * D), BF16), v((TILE, 8 * D), BF16),
            v((ROWS, 2 * D), BF16), v((ROWS, 2 * D), BF16), v((ROWS, 2 * D), BF16),
            v((2, ROWS), F32), v((2, NBLK, NBLK), jnp.int32),
            v((NBLK, BLOCK), jnp.int32), v((1, D), jnp.int32),
            v((2, NZ, PLANE, D), BF16),
            v((3, ROWS, 2 * D), BF16), v((3, ROWS, 2 * D), BF16),
            v((16, BLOCK), F32), v((3, 16, BLOCK), F32),
            v((2 * NBLK, NBLK), BF16), v((2 * NBLK, NBLK), BF16),
            v((2, 2 * NBLK, D), F32), v((8, D), jnp.int32),
            v((NZ, PLANE, D), BF16),
            v((2, 4, COLS, D), BF16), v((2, 4, COLS, D), BF16),
            v((2, 4, COLS, D), BF16), v((2, 4, COLS, D), BF16),
            v((2, NZ, PLANE, D), F32),
            v((2, 4, D, COLS), F32),
            v((2, 2, ROWS, 2 * D), F32),
            v((2, ROWS, 2 * D), F32), v((ROWS, 2 * D), BF16),
            v((2, 4, 4, HALF, D), BF16), v((2, 4, 4, HALF, D), BF16),
            v((8, 2, TILE, D), F32),
            v((TILE, COLS), jnp.int32),
            dma((9,)), dma((2, 8)), dma((2, 8)),
            dma((2, 4, 4)), dma((2, 4, 4)), dma((2, 4, 4)), dma((2, 4, 4)),
            dma((4,)), dma((4,)), dma((3,)), dma((3,)),
            dma((3,)), dma((3,)), dma((3,)), dma((3,)), dma((8,)), dma((8,)),
        ],
        compiler_params=pltpu.CompilerParams(
            collective_id=0, has_side_effects=True, vmem_limit_bytes=40 * MIB
        ),
    )(keys, values, queries, grads, outs, norms, layout, ids, jnp.pad(order, (0, D - NBLK)).reshape(1, D), order)


def finish_kernel(sums, pair_in, own_in, dq, dk, dv):
    dq[...] = sums[...] + pair_in[...].astype(F32)
    for g in range(8):
        dk[:, g * D : (g + 1) * D] = own_in[g, 0]
        dv[:, g * D : (g + 1) * D] = own_in[g, 1]


def finish(sums, pair_in, own_in):
    vmem = pl.BlockSpec(memory_space=pltpu.VMEM)
    return pl.pallas_call(
        finish_kernel,
        name="finish",
        out_shape=(
            jax.ShapeDtypeStruct((ROWS, 2 * D), F32),
            jax.ShapeDtypeStruct((TILE, 8 * D), F32),
            jax.ShapeDtypeStruct((TILE, 8 * D), F32),
        ),
        in_specs=[vmem] * 3,
        out_specs=(vmem,) * 3,
        compiler_params=pltpu.CompilerParams(vmem_limit_bytes=8 * MIB),
    )(sums, pair_in, own_in)


def body(
    queries, keys, values, attn_out, out_grad, log_norm, block_layout, document_ids, block_order
):
    return finish(
        *fused(
            keys,
            values,
            queries,
            out_grad,
            attn_out,
            log_norm,
            block_layout,
            document_ids.reshape(NBLK, BLOCK),
            block_order,
        )
    )


def solution(mesh):
    in_specs = (
        P("seq", "head"),
        P(("seq", "head"), None),
        P(("seq", "head"), None),
        P("seq", "head"),
        P("seq", "head"),
        P("head", "seq"),
        P("head", None, None),
        P(),
        P(),
    )
    out_specs = (P("seq", "head"), P(("seq", "head"), None), P(("seq", "head"), None))
    return jax.shard_map(body, mesh=mesh, in_specs=in_specs, out_specs=out_specs, check_vma=False)
```

time: 373 us -> 86.3 us (0.23); the launches traced: 368 us -> 85.9 us
  waiting for transfers between devices: 123 us -> 0 us
  matrix products: 116 us -> 0 us
  Pallas kernels: 0 us -> 77.7 us
  local copies, waits for them, and re-layouts: 67.5 us -> 7.46 us
  other arithmetic: 18.2 us -> 0 us
  starting transfers between devices: 17.9 us -> 0 us
  between operations: 14.3 us -> 0.66 us
  blocking collectives: 9.99 us -> 0 us
    dot_general x96 -> x0, matrix products: 116 us -> none  [the longest x16 33.7 us: block_grads(): jnp.einsum('hqk,qhd->kd', weights_low, grad_heads, preferred_element_type...]
    pallas_call x0 -> x2, Pallas kernels: none -> 77.7 us  [the longest x1 76.8 us: fused(): pl.pallas_call(fused_kernel, name='fused', out_shape=(jax.ShapeDtypeStruc...]
    reduce_scatter x1 -> x0, waiting for transfers between devices: 66.1 us -> none  [side_by_side(): lax.psum_scatter(both, axis, scatter_dimension=dim, tiled=True)]
    gather x17 -> x0, local copies, waits for them, and re-layouts: 53.4 us -> none  [lookup_rows(): return (position, jnp.take(document_ids, position), placed_hit)]
    all_gather x1 -> x0, waiting for transfers between devices: 38.2 us -> none  [in_one_piece(): lax.all_gather(both, axis, axis=dim, tiled=True)]
    all_to_all x3 -> x0, waiting for transfers between devices: 18.8 us -> none  [the longest x1 6.6 us: body(): lax.all_to_all(value_total, 'head', split_axis=0, concat_axis=1, tiled=True)]
    all_to_all x3 -> x0, starting transfers between devices: 17.8 us -> none  [the longest x1 7.57 us: body(): lax.all_to_all(widen(keys), 'head', split_axis=1, concat_axis=0, tiled=True)]
    all_to_all x1 -> x0, blocking collectives: 9.99 us -> none  [body(): lax.all_to_all(widen(values), 'head', split_axis=1, concat_axis=0, tiled=...]
  transfers between devices with their start and end apart: 5 -> 0, of which waited for: 5 -> 0; matrix products, arithmetic and copies ran while one was open for 2% -> 0% of each run, Pallas kernels for 0% -> 0%
where the time goes in v3:
time: 86.3 us; the launch traced here: 85.9 us
  Pallas kernels  77.7 us (90%)
  local copies, waits for them, and re-layouts  7.46 us (9%)
    pallas_call x1, Pallas kernels, fused(): pl.pallas_call(fused_kernel, name='fused', out_shape=(jax.ShapeDtypeStruc...  76.8 us
    unnamed x18, local copies, waits for them, and re-layouts  7.46 us

profile of v3, /device:TPU:1, one launch (start us, length us, event | category | flops | bytes accessed | tf_op | source)
XLA Modules:
  0.0 85.9 jit_solution(18114722518942850271)
XLA Ops:
  0.6 0.0 copy-start.8
  0.6 0.6 copy-done.8
  1.3 0.0 copy-start
  1.3 0.9 %copy-done = bf16[512,256]{1,0:T(8,128)(2,1)S(1)} copy-done((bf16[512,256]{1,0:T(8,128)(2,1)S(1)}, bf16[512,256]{1,0:T(8,128)(2,1)}, u32[]{:S(2)}) %copy-start) | copy-done | bytes 262168
  2.2 0.0 copy-start.1
  2.2 0.9 %copy-done.1 = bf16[512,256]{1,0:T(8,128)(2,1)S(1)} copy-done((bf16[512,256]{1,0:T(8,128)(2,1)S(1)}, bf16[512,256]{1,0:T(8,128)(2,1)}, u32[]{:S(2)}) %copy-start.1) | copy-done | bytes 262168
  3.2 0.0 copy-start.2
  3.2 0.9 %copy-done.2 = bf16[512,256]{1,0:T(8,128)(2,1)S(1)} copy-done((bf16[512,256]{1,0:T(8,128)(2,1)S(1)}, bf16[512,256]{1,0:T(8,128)(2,1)}, u32[]{:S(2)}) %copy-start.2) | copy-done | bytes 262168
  4.1 0.0 copy-start.3
  4.1 0.8 copy-done.3
  5.0 0.0 copy-start.4
  5.0 0.8 copy-done.4
  5.8 0.0 copy-start.5
  5.8 0.8 copy-done.5
  6.7 0.0 copy-start.6
  6.7 0.8 copy-done.6
  7.4 0.0 copy-start.7
  7.4 0.7 copy-done.7
  8.1 76.8 %fused.1 = (f32[512,256]{1,0:T(8,128)S(1)}, bf16[512,256]{1,0:T(8,128)(2,1)S(1)}, f32[8,2,32,128]{3,2,1,0:T(8,128)S(1)}) custom-call(bf16[32,1024]{1,0:T(8,128)(2,1)S(1)} %copy-done.3, bf16[32,1024]{1,0:T(8,128)(2,1)S(1)} %copy-done.4, bf16[512,256]{1,0:T(8,128)(2,1)S(1)} %copy-done, bf16[512,256]{1,0:T(8,128)(2,1)S(1)} %copy-done.1, ...), custom_call_target="tpu_custom_call" | custom-call | tf_op jit(solution)/shard_map/fused/pallas_call | solution.py:429
  84.9 0.9 %finish.1 = (f32[512,256]{1,0:T(8,128)}, f32[32,1024]{1,0:T(8,128)}, f32[32,1024]{1,0:T(8,128)}) custom-call(f32[512,256]{1,0:T(8,128)S(1)} %get-tuple-element.6.sums, bf16[512,256]{1,0:T(8,128)(2,1)S(1)} %get-tuple-element.7.pair_in, f32[8,2,32,128]{3,2,1,0:T(8,128)S(1)} %get-tuple-element.8.own_in), custom_call_target="tpu_custom_call" | custom-call | tf_op jit(solution)/shard_map/finish/pallas_call | solution.py:479
  (1 shorter events, 0.0 us)
Async XLA Ops:
  0.6 0.7 copy-start.8
  1.3 0.9 %copy-start = (bf16[512,256]{1,0:T(8,128)(2,1)S(1)}, bf16[512,256]{1,0:T(8,128)(2,1)}, u32[]{:S(2)}) copy-start(bf16[512,256]{1,0:T(8,128)(2,1)} %queries_h.1) | copy-start | bytes 786436
  2.2 0.9 %copy-start.1 = (bf16[512,256]{1,0:T(8,128)(2,1)S(1)}, bf16[512,256]{1,0:T(8,128)(2,1)}, u32[]{:S(2)}) copy-start(bf16[512,256]{1,0:T(8,128)(2,1)} %grads_h.1) | copy-start | bytes 786436
  3.2 0.9 %copy-start.2 = (bf16[512,256]{1,0:T(8,128)(2,1)S(1)}, bf16[512,256]{1,0:T(8,128)(2,1)}, u32[]{:S(2)}) copy-start(bf16[512,256]{1,0:T(8,128)(2,1)} %outs_h.1) | copy-start | bytes 786436
  4.1 0.8 copy-start.3
  5.0 0.8 copy-start.4
  5.8 0.8 copy-start.5
  6.7 0.8 copy-start.6
  7.4 0.7 copy-start.7

commit v4 on v3

v4 whole, which is shorter than its diff:
```python
import jax
import jax.numpy as jnp
from jax import lax
from jax.experimental import pallas as pl
from jax.experimental.pallas import tpu as pltpu
from jax.sharding import PartitionSpec as P

MESH = pl.DeviceIdType.MESH
D = 128
BLOCK = 128
NBLK = 64
NZ = 8
TILE = 32
TILES = 8
PLANE = TILE * TILES
ROWS = 512
COLS = 512
BIG = 1e30
ALWAYS = 1 << 20
SCALE = D ** (-0.5)
LOG2E = 1.4426950408889634
BF16 = jnp.bfloat16
F32 = jnp.float32
NN = (((1,), (0,)), ((), ()))
NT = (((1,), (1,)), ((), ()))
TN = (((0,), (0,)), ((), ()))
AT_DOC = 64
AT_ONE = 72
MIB = 1 << 20


def place():
    s = lax.axis_index("seq")
    h = lax.axis_index("head")
    return s, h, s // 2, s % 2, h // 4, h % 4


def send(src, dst, send_sem, recv_sem, seq, head):
    return pltpu.make_async_remote_copy(
        src_ref=src,
        dst_ref=dst,
        send_sem=send_sem,
        recv_sem=recv_sem,
        device_id=(seq, head),
        device_id_type=MESH,
    )


def dot(a, b, dims):
    return lax.dot_general(a, b, dims, preferred_element_type=F32)


def three(x):
    high = x.astype(BF16)
    rest = x - high.astype(F32)
    mid = rest.astype(BF16)
    low = (rest - mid.astype(F32)).astype(BF16)
    return [high, mid, low]


def iota(shape, dim):
    return lax.broadcasted_iota(jnp.int32, shape, dim)


def fused_kernel(
    keys_h, values_h, queries_h, grads_h, outs_h, norms_h, layout_h, ids_h, order_h,
    dq, pair_in, own_in,
    keys, values, queries, grads, outs, norms, layout, ids, order, order_v,
    kv, qt, gt, st, lay, l_in, lperm, spans, docs,
    ax, qx, gx, lows, sgs, acc, dqt, dqp, twin_in, pair_out, z_out, z_in, fin, ahead, pick,
    l_sem, a_send, a_recv, k_send, k_recv, z_send, z_recv, y_send, y_recv, d_send, d_recv,
    f_send, f_recv, r_send, r_recv, b_send, b_recv,
):
    s, h, z, c, x, y = place()
    pair = h + 1 - 2 * (y % 2)
    twin = s + 1 - 2 * c
    up = ((z + 1) % NZ) * 2 + c
    down = ((z + NZ - 1) % NZ) * 2 + c
    hp = y % 2
    quarter = hp * 2 + c

    loads = []
    for i, (src, dst) in enumerate((
        (queries_h, queries), (keys_h, keys), (values_h, values), (grads_h, grads), (outs_h, outs),
        (norms_h, norms), (layout_h, layout), (ids_h, ids), (order_h, order),
    )):
        loads.append(pltpu.make_async_copy(src, dst, l_sem.at[i]))
        loads[i].start()

    takers, givers = [], []
    for xg in range(4):
        for yp in range(2):
            seq, head = z * 2 + y % 2, xg * 4 + yp * 2 + y // 2
            takers.append((seq, head, (seq != s) | (head != h)))
    for cg in range(2):
        for xg in range(4):
            seq, head = z * 2 + cg, xg * 4 + quarter
            givers.append((seq, head, (seq != s) | (head != h)))
    barrier = pltpu.get_barrier_semaphore()
    for seq, head in ((s, pair), (twin, h), (up, h), (down, h)):
        pl.semaphore_signal(barrier, inc=1, device_id=(seq, head), device_id_type=MESH)
    for seq, head, other in takers + givers:

        @pl.when(other)
        def _():
            pl.semaphore_signal(barrier, inc=1, device_id=(seq, head), device_id_type=MESH)

    above = [(z + d) % NZ for d in range(5)]
    under = [(z + NZ - d) % NZ for d in range(5)]
    own = ((y % 2 == c) & (y // 2 == hp)).astype(jnp.int32)
    mine = pl.ds(c * 2, 2)

    def columns(source, target):
        for rb in range(4):
            for hh in range(2):
                at = (rb % 2 * 2 + hh) * BLOCK
                block = source[rb * BLOCK : (rb + 1) * BLOCK, hh * D : (hh + 1) * D]
                target[0, c * 2 + rb // 2, :, at : at + BLOCK] = block.T

    loads[0].wait()
    columns(queries, qt)
    for load in loads[1:4]:
        load.wait()
    columns(grads, gt)
    pl.semaphore_wait(barrier, 4 + 16 - 2 * own)

    slot = c * 4 + x
    slot_rows = pl.ds(pl.multiple_of(slot * TILE, TILE), TILE)
    a_copies = []
    for t, src in enumerate((keys, values)):
        for g, (seq, head, other) in enumerate(takers):
            copy = send(
                src.at[:, pl.ds(g * D, D)], kv.at[t, z, slot_rows, :],
                a_send.at[t, g], a_recv.at[t, slot], seq, head,
            )
            pl.when(other)(copy.start)
            a_copies.append((copy, other))

            @pl.when(jnp.logical_not(other))
            def _():
                kv[t, z, slot_rows, :] = src[:, g * D : (g + 1) * D]

    def y_copy(k):
        src = (qt.at[0, mine], gt.at[0, mine], lay, st.at[0, c])[k]
        dst = (qt.at[1, mine], gt.at[1, mine], l_in, st.at[1, c])[k]
        return send(src, dst, y_send.at[k], y_recv.at[k], s, pair)

    d_copies = [
        send(qt.at[0, mine], qt.at[0, mine], d_send.at[0], d_recv.at[0], twin, h),
        send(gt.at[0, mine], gt.at[0, mine], d_send.at[1], d_recv.at[1], twin, h),
        send(st.at[0, c], st.at[0, c], d_send.at[2], d_recv.at[2], twin, h),
    ]
    for copy in (y_copy(0), d_copies[0], d_copies[1], y_copy(1)):
        copy.start()
    for load in loads[4:]:
        load.wait()

    ones = jnp.ones((8, D), BF16)
    for hh in range(2):
        lay[hh * NBLK : (hh + 1) * NBLK, :] = layout[hh].astype(F32).astype(BF16)
        for rb in range(4):
            at = (slice(rb * BLOCK, (rb + 1) * BLOCK), slice(hh * D, (hh + 1) * D))
            product = grads[at].astype(F32) * outs[at].astype(F32)
            high = product.astype(BF16)
            low = (product - high.astype(F32)).astype(BF16)
            total = dot(ones, high, NT) + dot(ones, low, NT)
            row = hh * 4 + rb
            st[0, c, row : row + 1, :] = norms[hh : hh + 1, rb * BLOCK : (rb + 1) * BLOCK]
            st[0, c, 8 + row : 9 + row, :] = total[0:1, :]
    for copy in (y_copy(3), d_copies[2], y_copy(2)):
        copy.start()
    acc[...] = jnp.zeros_like(acc)
    dqt[...] = jnp.zeros_like(dqt)
    qx[...] = jnp.zeros_like(qx)
    gx[...] = jnp.zeros_like(gx)
    pick[...] = jnp.zeros_like(pick)

    lane = iota((1, D), 1)
    placed = jnp.zeros((1, D), jnp.int32)
    for sb in range(NBLK):
        placed = jnp.where(lane == sb, order[sb], placed)
    order_v[...] = placed
    first, after = jnp.zeros((1, D), F32), jnp.full((1, D), float(ALWAYS), F32)
    row8 = iota((8, COLS), 0)
    first_row, after_row = jnp.zeros((8, COLS), F32), jnp.full((8, COLS), float(ALWAYS), F32)
    for d in range(1, 8):
        below = jnp.sum((ids[...] < d).astype(F32), axis=(0, 1), keepdims=True)
        first = jnp.where(lane == AT_DOC + d, below, first)
        after = jnp.where(lane == AT_DOC + d - 1, below, after)
        first_row = jnp.where(row8 == d, below, first_row)
        after_row = jnp.where(row8 == d - 1, below, after_row)
    spans[0:1, :] = first.astype(jnp.int32)
    spans[1:2, :] = after.astype(jnp.int32)
    docs[0] = first_row.astype(jnp.int32)
    docs[1] = after_row.astype(jnp.int32)

    stored = (iota((NBLK, D), 0) == order_v[...]) & (iota((NBLK, D), 1) < NBLK)
    stored = stored.astype(F32).astype(BF16)
    lperm[0] = dot(lay[...], stored, NN)
    ahead[...] = quarter * TILE + iota((TILE, COLS), 0) - iota((TILE, COLS), 1) % BLOCK
    spread = (iota((8, COLS), 1) // BLOCK == iota((8, COLS), 0)).astype(F32)
    doc_lane = (lane >= AT_DOC) & (lane < AT_ONE)

    def prepare(side, cb):
        for rp in range(2):
            unit = cb * 2 + rp
            norm, delta, position = [], [], []
            for b in range(2):
                block = order[z * 8 + unit * 2 + b]
                for hh in range(2):
                    at, row = b * 2 + hh, hh * 4 + rp * 2 + b
                    norm.append(st[side, cb, row : row + 1, :])
                    delta.append(st[side, cb, 8 + row : 9 + row, :])
                    position.append(block * BLOCK + iota((1, BLOCK), 1))
                    seen = lperm[side, pl.ds(hh * NBLK + block, 1), :]
                    pick[at : at + 1, :] = jnp.where((seen > 0.5) & (order_v[...] <= block), 1.0, 0.0)
            norm = three(jnp.concatenate(norm, axis=1) * (-1.0 / SCALE))
            delta = three(-jnp.concatenate(delta, axis=1))
            position = jnp.concatenate(position, axis=1)
            seen = dot(pick[...], spread, TN)
            qx[side, unit, 0:NBLK, :] = jnp.where(seen[0:NBLK, :] > 0.5, 0.0, -BIG).astype(BF16)
            inside = (position >= docs[0]) & (position < docs[1])
            zero = jnp.zeros((8, COLS), F32)
            for ref, rows, head in ((qx, norm, jnp.where(inside, 0.0, -BIG)), (gx, delta, zero)):
                parts = zero
                for i in range(3):
                    parts = jnp.where(row8 == i, rows[i].astype(F32), parts)
                ref[side, unit, AT_DOC : AT_DOC + 16, :] = jnp.concatenate([head, parts], axis=0).astype(BF16)

    def prepare_keys(plane):
        row, col = iota((TILE, D), 0), iota((TILE, D), 1)
        for t in range(TILES):
            position = order[plane * TILES + t] * BLOCK + quarter * TILE + row
            hot = col == plane * TILES + t
            hot = hot | (doc_lane & (position >= spans[0:1, :]) & (position < spans[1:2, :]))
            hot = hot | ((col >= AT_ONE) & (col < AT_ONE + 3))
            ax[plane, pl.ds(t * TILE, TILE), :] = hot.astype(F32).astype(BF16)

    def spot(n):
        side = n // 32
        j = n % 32 // 4
        j = j + side * (7 - 2 * j)
        away = (j + 1) // 2
        return (z + NZ + away * (1 - 2 * (j % 2))) % NZ, side, n % 4

    def front(n):
        plane, side, unit = spot(n)
        extra = ax[plane]
        scores = dot(
            jnp.concatenate([kv[0, plane], extra], 1), jnp.concatenate([qt[side, unit], qx[side, unit]], 0), NN
        )
        grads_less = dot(
            jnp.concatenate([kv[1, plane], extra], 1), jnp.concatenate([gt[side, unit], gx[side, unit]], 0), NN
        )
        low, score_grad = [], []
        for t in range(TILES):
            part = slice(t * TILE, (t + 1) * TILE)
            bound = []
            for b in range(2):
                same = order[plane * TILES + t] == order[z * 8 + unit * 2 + b]
                bound.append(jnp.full((1, 2 * BLOCK), jnp.where(same, 0, ALWAYS), jnp.int32))
            visible = ahead[...] <= jnp.concatenate(bound, axis=1)
            weights = jnp.where(visible, jnp.exp2(scores[part, :] * (SCALE * LOG2E)), 0.0)
            low.append(weights.astype(BF16))
            score_grad.append((weights * grads_less[part, :]).astype(BF16))
        return jnp.concatenate(low, axis=0), jnp.concatenate(score_grad, axis=0)

    def back(n, low, score_grad):
        plane, side, unit = spot(n)
        acc[0, plane] += dot(qt[side, unit], score_grad, NT)
        acc[1, plane] += dot(gt[side, unit], low, NT)
        dqt[side, unit] += dot(kv[0, plane], score_grad, TN)

    def query_sums(side, cb):
        for rb in range(4):
            for hh in range(2):
                at = (rb % 2 * 2 + hh) * BLOCK
                block_grad = dqt[side, cb * 2 + rb // 2, :, at : at + BLOCK].T * SCALE
                dqp[side, cb, rb * BLOCK : (rb + 1) * BLOCK, hh * D : (hh + 1) * D] = block_grad

    def key_copy(way, step, t):
        piece = kv.at[t, under[step - 1] if way == 0 else above[step - 1]]
        return send(
            piece, piece, k_send.at[way, step - 1, t], k_recv.at[way, step - 1, t],
            up if way == 0 else down, h,
        )

    def carries(way, step, t):
        return step < 4 or (step == 4 and t == way)

    def arrive(step, t):
        for way in range(2):
            if carries(way, step, t):
                key_copy(way, step, t).wait_recv()
            if carries(way, step + 1, t):
                key_copy(way, step + 1, t).start()

    for t in range(2):
        for at, (seq, head, other) in enumerate(givers):
            landed = send(
                keys.at[:, pl.ds(0, D)], kv.at[t, z, pl.ds(at * TILE, TILE), :],
                a_send.at[t, 0], a_recv.at[t, at], seq, head,
            )
            pl.when(other)(landed.wait_recv)
        for way in range(2):
            key_copy(way, 1, t).start()

    def forward(k):
        src = (qt.at[1, mine], gt.at[1, mine], None, st.at[1, c])[k]
        return send(src, src, f_send.at[k], f_recv.at[k], twin, h)

    def pass_on(k):
        y_copy(k).wait_recv()
        forward(k).start()

    def sum_copy(way, step, t):
        return send(
            z_out.at[way, step - 1, t], z_in.at[way, step - 1, t],
            z_send.at[way, step - 1, t], z_recv.at[way, step - 1, t],
            up if way == 0 else down, h,
        )

    def pass_sum(way, step, t):
        value = acc[t, (above if way == 0 else under)[5 - step]]
        if step > 2 or (step == 2 and t == way):
            sum_copy(way, step - 1, t).wait_recv()
            value = value + z_in[way, step - 2, t].astype(F32)
        z_out[way, step - 1, t] = value.astype(BF16)
        sum_copy(way, step, t).start()

    def twin_copy(side):
        return send(dqp.at[side, 1 - c], twin_in.at[side], r_send.at[side], r_recv.at[side], twin, h)

    def twin_sums(side):
        query_sums(side, 1 - c)
        twin_copy(side).start()

    prepare(0, c)
    prepare_keys(z)
    for copy in d_copies:
        copy.wait_recv()
    prepare(0, 1 - c)
    lows[0], sgs[0] = front(0)

    def planes_at(away):
        prepare_keys(under[away])
        if away < 4:
            prepare_keys(above[away])

    def heads_come():
        pass_on(1)
        pass_on(3)
        y_copy(2).wait_recv()

    def other_heads():
        lperm[1] = dot(l_in[...], stored, NN)
        prepare(1, c)
        for k in (0, 1, 3):
            forward(k).wait_recv()
        prepare(1, 1 - c)

    def sums(*which):
        for w in which:
            pass_sum(*w)

    events = {
        1: lambda: (planes_at(1), arrive(1, 0), arrive(1, 1)),
        3: lambda: (planes_at(2), arrive(2, 0), pass_on(0)),
        5: lambda: arrive(2, 1),
        7: lambda: (planes_at(3), arrive(3, 0)),
        9: lambda: (arrive(3, 1), heads_come()),
        11: lambda: (planes_at(4), arrive(4, 0)),
        13: lambda: (other_heads(), arrive(4, 1)),
        21: lambda: twin_sums(0),
        18: lambda: sums((0, 1, 0), (1, 1, 1)),
        20: lambda: sums((0, 2, 1)),
        22: lambda: sums((1, 2, 0)),
        24: lambda: sums((0, 2, 0), (1, 2, 1)),
        26: lambda: sums((0, 3, 1)),
        28: lambda: sums((1, 3, 0)),
        30: lambda: sums((0, 3, 0), (1, 3, 1)),
    }

    def two(i, _):
        for at, event in events.items():
            pl.when(i == at)(lambda event=event: (event(), None)[1])
        n = 2 * i
        lows[1], sgs[1] = front(n + 1)
        back(n, lows[0], sgs[0])
        lows[0], sgs[0] = front(jnp.minimum(n + 2, 63))
        back(n + 1, lows[1], sgs[1])
        return 0

    lax.fori_loop(0, 32, two, 0)

    twin_sums(1)
    sums((0, 4, 1), (1, 4, 0))
    query_sums(1, c)
    twin_copy(1).wait_recv()
    pair_out[...] = (dqp[1, c] + twin_in[1]).astype(BF16)
    pair_copy = send(pair_out, pair_in, r_send.at[2], r_recv.at[2], s, pair)
    pair_copy.start()
    sums((0, 4, 0), (1, 4, 1))
    query_sums(0, c)
    twin_copy(0).wait_recv()
    dq[...] = dqp[0, c] + twin_in[0]

    b_copies = []
    g = x * 2 + y // 2
    for t in (1, 0):
        value = acc[t, z]
        for way in (0, 1):
            sum_copy(way, 4, t).wait_recv()
            value = value + z_in[way, 3, t].astype(F32)
        if t == 0:
            value = value * SCALE
        value = value.T
        for k in range(8):
            fin[k, t] = value[k * TILE : (k + 1) * TILE, :]
    for k, (seq, head, other) in enumerate(givers):
        copy = send(fin.at[k], own_in.at[g], b_send.at[k], b_recv.at[g], seq, head)
        pl.when(other)(copy.start)
        b_copies.append((copy, other))

        @pl.when(jnp.logical_not(other))
        def _():
            own_in[g] = fin[k]

    for g, (seq, head, other) in enumerate(takers):
        landed = send(fin.at[0], own_in.at[g], b_send.at[0], b_recv.at[g], seq, head)
        pl.when(other)(landed.wait_recv)
    pair_copy.wait_recv()

    for copy, other in a_copies + b_copies:
        pl.when(other)(copy.wait_send)
    for way in range(2):
        for t in range(2):
            for step in range(1, 5):
                if carries(way, step, t):
                    key_copy(way, step, t).wait_send()
                if step > 1 or t == way:
                    sum_copy(way, step, t).wait_send()
    for k in range(4):
        y_copy(k).wait_send()
        if k != 2:
            forward(k).wait_send()
    for copy in d_copies + [twin_copy(0), twin_copy(1), pair_copy]:
        copy.wait_send()


def fused(keys, values, queries, grads, outs, norms, layout, ids, order):
    vmem = pl.BlockSpec(memory_space=pltpu.VMEM)
    hbm = pl.BlockSpec(memory_space=pltpu.HBM)
    dma = pltpu.SemaphoreType.DMA
    v = pltpu.VMEM
    return pl.pallas_call(
        fused_kernel,
        name="fused",
        out_shape=(
            jax.ShapeDtypeStruct((ROWS, 2 * D), F32),
            jax.ShapeDtypeStruct((ROWS, 2 * D), BF16),
            jax.ShapeDtypeStruct((8, 2, TILE, D), F32),
        ),
        in_specs=[hbm] * 9,
        out_specs=(vmem,) * 3,
        scratch_shapes=[
            v((TILE, 8 * D), BF16), v((TILE, 8 * D), BF16),
            v((ROWS, 2 * D), BF16), v((ROWS, 2 * D), BF16), v((ROWS, 2 * D), BF16),
            v((2, ROWS), F32), v((2, NBLK, NBLK), jnp.int32),
            v((NBLK, BLOCK), jnp.int32), pltpu.SMEM((NBLK,), jnp.int32), v((1, D), jnp.int32),
            v((2, NZ, PLANE, D), BF16),
            v((2, 4, D, COLS), BF16), v((2, 4, D, COLS), BF16),
            v((2, 2, 16, BLOCK), F32),
            v((2 * NBLK, NBLK), BF16), v((2 * NBLK, NBLK), BF16),
            v((2, 2 * NBLK, D), F32), v((8, D), jnp.int32), v((2, 8, COLS), jnp.int32),
            v((NZ, PLANE, D), BF16),
            v((2, 4, D, COLS), BF16), v((2, 4, D, COLS), BF16),
            v((2, PLANE, COLS), BF16), v((2, PLANE, COLS), BF16),
            v((2, NZ, D, PLANE), F32),
            v((2, 4, D, COLS), F32),
            v((2, 2, ROWS, 2 * D), F32),
            v((2, ROWS, 2 * D), F32), v((ROWS, 2 * D), BF16),
            v((2, 4, 2, D, PLANE), BF16), v((2, 4, 2, D, PLANE), BF16),
            v((8, 2, TILE, D), F32),
            v((TILE, COLS), jnp.int32), v((8, D), F32),
            dma((9,)), dma((2, 8)), dma((2, 8)),
            dma((2, 4, 2)), dma((2, 4, 2)), dma((2, 4, 2)), dma((2, 4, 2)),
            dma((4,)), dma((4,)), dma((3,)), dma((3,)),
            dma((4,)), dma((4,)), dma((3,)), dma((3,)), dma((8,)), dma((8,)),
        ],
        compiler_params=pltpu.CompilerParams(
            collective_id=0, has_side_effects=True, vmem_limit_bytes=60 * MIB
        ),
    )(keys, values, queries, grads, outs, norms, layout, ids, order)


def finish_kernel(sums, pair_in, own_in, dq, dk, dv):
    dq[...] = sums[...] + pair_in[...].astype(F32)
    for g in range(8):
        dk[:, g * D : (g + 1) * D] = own_in[g, 0]
        dv[:, g * D : (g + 1) * D] = own_in[g, 1]


def finish(sums, pair_in, own_in):
    vmem = pl.BlockSpec(memory_space=pltpu.VMEM)
    return pl.pallas_call(
        finish_kernel,
        name="finish",
        out_shape=(
            jax.ShapeDtypeStruct((ROWS, 2 * D), F32),
            jax.ShapeDtypeStruct((TILE, 8 * D), F32),
            jax.ShapeDtypeStruct((TILE, 8 * D), F32),
        ),
        in_specs=[vmem] * 3,
        out_specs=(vmem,) * 3,
        compiler_params=pltpu.CompilerParams(vmem_limit_bytes=60 * MIB),
    )(sums, pair_in, own_in)


def body(
    queries, keys, values, attn_out, out_grad, log_norm, block_layout, document_ids, block_order
):
    return finish(
        *fused(
            keys,
            values,
            queries,
            out_grad,
            attn_out,
            log_norm,
            block_layout,
            document_ids.reshape(NBLK, BLOCK),
            block_order,
        )
    )


def solution(mesh):
    in_specs = (
        P("seq", "head"),
        P(("seq", "head"), None),
        P(("seq", "head"), None),
        P("seq", "head"),
        P("seq", "head"),
        P("head", "seq"),
        P("head", None, None),
        P(),
        P(),
    )
    out_specs = (P("seq", "head"), P(("seq", "head"), None), P(("seq", "head"), None))
    return jax.shard_map(body, mesh=mesh, in_specs=in_specs, out_specs=out_specs, check_vma=False)
```

time: 86.3 us -> 69.7 us (0.81)
  Pallas kernels: 77.7 us -> 68.9 us
  local copies, waits for them, and re-layouts: 7.46 us -> 0 us
    pallas_call x1, Pallas kernels: 76.8 us -> 66.8 us  [fused(): pl.pallas_call(fused_kernel, name='fused', out_shape=(jax.ShapeDtypeStruc...]
    unnamed x18 -> x0, local copies, waits for them, and re-layouts: 7.46 us -> none
    pallas_call x1, Pallas kernels: 0.93 us -> 2.07 us  [finish(): pl.pallas_call(finish_kernel, name='finish', out_shape=(jax.ShapeDtypeStr...]
where the time goes in v4:
time: 69.7 us; the launch traced here: 69.6 us
  Pallas kernels  68.9 us (99%)
    pallas_call x1, Pallas kernels, fused(): pl.pallas_call(fused_kernel, name='fused', out_shape=(jax.ShapeDtypeStruc...  66.8 us
    pallas_call x1, Pallas kernels, finish(): pl.pallas_call(finish_kernel, name='finish', out_shape=(jax.ShapeDtypeStr...  2.07 us

profile of v4, /device:TPU:1, one launch (start us, length us, event | category | flops | bytes accessed | tf_op | source)
XLA Modules:
  0.0 69.6 jit_solution(17090315313846554755)
XLA Ops:
  0.6 66.8 %fused.1 = (f32[512,256]{1,0:T(8,128)}, bf16[512,256]{1,0:T(8,128)(2,1)}, f32[8,2,32,128]{3,2,1,0:T(8,128)}) custom-call(bf16[32,1024]{1,0:T(8,128)(2,1)} %keys_h.1, bf16[32,1024]{1,0:T(8,128)(2,1)} %values_h.1, bf16[512,256]{1,0:T(8,128)(2,1)} %queries_h.1, bf16[512,256]{1,0:T(8,128)(2,1)} %grads_h.1, bf16[512,256]{1,0:T(8,128)(2,1)} %outs_h.1, ...), custom_call_target="tpu_custom_call" | custom-call | tf_op jit(solution)/shard_map/fused/pallas_call | solution.py:456
  67.5 2.1 %finish.1 = (f32[512,256]{1,0:T(8,128)}, f32[32,1024]{1,0:T(8,128)}, f32[32,1024]{1,0:T(8,128)}) custom-call(f32[512,256]{1,0:T(8,128)} %get-tuple-element.6.sums, bf16[512,256]{1,0:T(8,128)(2,1)} %get-tuple-element.7.pair_in, f32[8,2,32,128]{3,2,1,0:T(8,128)} %get-tuple-element.8.own_in), custom_call_target="tpu_custom_call" | custom-call | tf_op jit(solution)/shard_map/finish/pallas_call | solution.py:506

commit v5 on v4

--- a/solution.py
+++ b/solution.py
@@ -64,12 +64,12 @@
 
 def fused_kernel(
     keys_h, values_h, queries_h, grads_h, outs_h, norms_h, layout_h, ids_h, order_h,
-    dq, pair_in, own_in,
+    dq, pair_in, own_in, way_in,
     keys, values, queries, grads, outs, norms, layout, ids, order, order_v,
     kv, qt, gt, st, lay, l_in, lperm, spans, docs,
-    ax, qx, gx, lows, sgs, acc, dqt, dqp, twin_in, pair_out, z_out, z_in, fin, ahead, pick,
+    ax, qx, gx, lows, sgs, acc, dqt, dqp, twin_in, pair_out, z_out, z_in, fin, fin_way, ahead, pick,
     l_sem, a_send, a_recv, k_send, k_recv, z_send, z_recv, y_send, y_recv, d_send, d_recv,
-    f_send, f_recv, r_send, r_recv, b_send, b_recv,
+    f_send, f_recv, r_send, r_recv, b_send, b_recv, w_send, w_recv,
 ):
     s, h, z, c, x, y = place()
     pair = h + 1 - 2 * (y % 2)
@@ -77,7 +77,8 @@
     up = ((z + 1) % NZ) * 2 + c
     down = ((z + NZ - 1) % NZ) * 2 + c
     hp = y % 2
-    quarter = hp * 2 + c
+    inner = (y + 1) // 2 % 2
+    quarter = inner + c * (3 - 2 * inner)
 
     loads = []
     for i, (src, dst) in enumerate((
@@ -87,27 +88,37 @@
         loads.append(pltpu.make_async_copy(src, dst, l_sem.at[i]))
         loads[i].start()
 
-    takers, givers = [], []
-    for xg in range(4):
-        for yp in range(2):
-            seq, head = z * 2 + y % 2, xg * 4 + yp * 2 + y // 2
-            takers.append((seq, head, (seq != s) | (head != h)))
-    for cg in range(2):
+    above = [(z + d) % NZ for d in range(5)]
+    under = [(z + NZ - d) % NZ for d in range(5)]
+    own = (y // 2 == c).astype(jnp.int32)
+
+    def takers(plane):
+        out = []
         for xg in range(4):
-            seq, head = z * 2 + cg, xg * 4 + quarter
-            givers.append((seq, head, (seq != s) | (head != h)))
+            for yp in range(2):
+                head = xg * 4 + (inner if yp == 0 else 3 - inner)
+                out.append((plane * 2 + y // 2, head, (plane * 2 + y // 2 != s) | (head != h)))
+        return out
+
+    def givers(plane):
+        out = []
+        for cg in range(2):
+            for xg in range(4):
+                seq, head = plane * 2 + cg, xg * 4 + quarter
+                out.append((seq, head, (seq != s) | (head != h)))
+        return out
+
+    near = (z, above[1], under[1])
     barrier = pltpu.get_barrier_semaphore()
     for seq, head in ((s, pair), (twin, h), (up, h), (down, h)):
         pl.semaphore_signal(barrier, inc=1, device_id=(seq, head), device_id_type=MESH)
-    for seq, head, other in takers + givers:
-
-        @pl.when(other)
-        def _():
-            pl.semaphore_signal(barrier, inc=1, device_id=(seq, head), device_id_type=MESH)
-
-    above = [(z + d) % NZ for d in range(5)]
-    under = [(z + NZ - d) % NZ for d in range(5)]
-    own = ((y % 2 == c) & (y // 2 == hp)).astype(jnp.int32)
+    for plane in near:
+        for seq, head, other in takers(plane) + givers(plane):
+
+            @pl.when(other)
+            def _():
+                pl.semaphore_signal(barrier, inc=1, device_id=(seq, head), device_id_type=MESH)
+
     mine = pl.ds(c * 2, 2)
 
     def columns(source, target):
@@ -122,23 +133,34 @@
     for load in loads[1:4]:
         load.wait()
     columns(grads, gt)
-    pl.semaphore_wait(barrier, 4 + 16 - 2 * own)
+    pl.semaphore_wait(barrier, 4 + 48 - 2 * own)
 
     slot = c * 4 + x
     slot_rows = pl.ds(pl.multiple_of(slot * TILE, TILE), TILE)
-    a_copies = []
-    for t, src in enumerate((keys, values)):
-        for g, (seq, head, other) in enumerate(takers):
-            copy = send(
-                src.at[:, pl.ds(g * D, D)], kv.at[t, z, slot_rows, :],
-                a_send.at[t, g], a_recv.at[t, slot], seq, head,
+
+    def row_copy(o, t, g, seq, head):
+        return send(
+            (keys, values)[t].at[:, pl.ds(g * D, D)], kv.at[t, z, slot_rows, :],
+            a_send.at[o, t, g], a_recv.at[o, t, slot], seq, head,
+        )
+
+    for t in range(2):
+        for o, plane in enumerate(near):
+            for g, (seq, head, other) in enumerate(takers(plane)):
+                pl.when(other)(row_copy(o, t, g, seq, head).start)
+
+                @pl.when(jnp.logical_not(other))
+                def _():
+                    kv[t, z, slot_rows, :] = (keys, values)[t][:, g * D : (g + 1) * D]
+
+    def rows_come(o, t):
+        plane = (z, under[1], above[1])[o]
+        for at, (seq, head, other) in enumerate(givers(plane)):
+            landed = send(
+                keys.at[:, pl.ds(0, D)], kv.at[t, plane, pl.ds(at * TILE, TILE), :],
+                a_send.at[o, t, 0], a_recv.at[o, t, at], seq, head,
             )
-            pl.when(other)(copy.start)
-            a_copies.append((copy, other))
-
-            @pl.when(jnp.logical_not(other))
-            def _():
-                kv[t, z, slot_rows, :] = src[:, g * D : (g + 1) * D]
+            pl.when(other)(landed.wait_recv)
 
     def y_copy(k):
         src = (qt.at[0, mine], gt.at[0, mine], lay, st.at[0, c])[k]
@@ -240,8 +262,14 @@
         side = n // 32
         j = n % 32 // 4
         j = j + side * (7 - 2 * j)
+        unit = n % 4
+        m = n - 52
+        late = jnp.where(m >= 0, 1, 0)
+        k = m // 3
+        j = j + late * (2 - m % 3 - j)
+        unit = unit + late * ((k // 2 * (2 * c - 1) + 1 - c) * 2 + k % 2 - unit)
         away = (j + 1) // 2
-        return (z + NZ + away * (1 - 2 * (j % 2))) % NZ, side, n % 4
+        return (z + NZ + away * (1 - 2 * (j % 2))) % NZ, side, unit
 
     def front(n):
         plane, side, unit = spot(n)
@@ -271,8 +299,8 @@
         acc[1, plane] += dot(gt[side, unit], low, NT)
         dqt[side, unit] += dot(kv[0, plane], score_grad, TN)
 
-    def query_sums(side, cb):
-        for rb in range(4):
+    def query_sums(side, cb, blocks=range(4)):
+        for rb in blocks:
             for hh in range(2):
                 at = (rb % 2 * 2 + hh) * BLOCK
                 block_grad = dqt[side, cb * 2 + rb // 2, :, at : at + BLOCK].T * SCALE
@@ -294,16 +322,6 @@
                 key_copy(way, step, t).wait_recv()
             if carries(way, step + 1, t):
                 key_copy(way, step + 1, t).start()
-
-    for t in range(2):
-        for at, (seq, head, other) in enumerate(givers):
-            landed = send(
-                keys.at[:, pl.ds(0, D)], kv.at[t, z, pl.ds(at * TILE, TILE), :],
-                a_send.at[t, 0], a_recv.at[t, at], seq, head,
-            )
-            pl.when(other)(landed.wait_recv)
-        for way in range(2):
-            key_copy(way, 1, t).start()
 
     def forward(k):
         src = (qt.at[1, mine], gt.at[1, mine], None, st.at[1, c])[k]
@@ -335,12 +353,49 @@
         query_sums(side, 1 - c)
         twin_copy(side).start()
 
+    def pair_copy(rp):
+        rows = pl.ds(rp * 2 * BLOCK, 2 * BLOCK)
+        return send(
+            pair_out.at[rows, :], pair_in.at[rows, :], r_send.at[2 + rp], r_recv.at[2 + rp], s, pair
+        )
+
+    def pair_sums(rp):
+        query_sums(1, c, range(rp * 2, rp * 2 + 2))
+        if rp == 0:
+            twin_copy(1).wait_recv()
+        rows = slice(rp * 2 * BLOCK, (rp + 1) * 2 * BLOCK)
+        pair_out[rows, :] = (dqp[1, c, rows, :] + twin_in[1, rows, :]).astype(BF16)
+        pair_copy(rp).start()
+
+    mine_g = x * 2 + y // 2
+
+    def way_copy(way, t, k, seq, head):
+        return send(
+            fin_way.at[way, k, t], way_in.at[way, mine_g, t],
+            w_send.at[way, t, k], w_recv.at[way, t, mine_g], seq, head,
+        )
+
+    def last_sum(way, t):
+        plane = (above if way == 0 else under)[1]
+        sum_copy(way, 3, t).wait_recv()
+        value = (acc[t, plane] + z_in[way, 2, t].astype(F32)).T.astype(BF16)
+        for k, (seq, head, _) in enumerate(givers(plane)):
+            fin_way[way, k, t] = value[k * TILE : (k + 1) * TILE, :]
+        for k, (seq, head, _) in enumerate(givers(plane)):
+            way_copy(way, t, k, seq, head).start()
+
     prepare(0, c)
-    prepare_keys(z)
+    for plane in near:
+        prepare_keys(plane)
     for copy in d_copies:
         copy.wait_recv()
     prepare(0, 1 - c)
-    lows[0], sgs[0] = front(0)
+    for t in range(2):
+        rows_come(0, t)
+        for way in range(2):
+            rows_come(1 + way, t)
+            key_copy(way, 2, t).start()
+    lows[0], sgs[0] = front(z * 0)
 
     def planes_at(away):
         prepare_keys(under[away])
@@ -364,21 +419,23 @@
             pass_sum(*w)
 
     events = {
-        1: lambda: (planes_at(1), arrive(1, 0), arrive(1, 1)),
-        3: lambda: (planes_at(2), arrive(2, 0), pass_on(0)),
+        4: lambda: (planes_at(2), arrive(2, 0)),
         5: lambda: arrive(2, 1),
-        7: lambda: (planes_at(3), arrive(3, 0)),
-        9: lambda: (arrive(3, 1), heads_come()),
+        6: lambda: pass_on(0),
+        8: lambda: (planes_at(3), arrive(3, 0)),
+        9: lambda: arrive(3, 1),
         11: lambda: (planes_at(4), arrive(4, 0)),
-        13: lambda: (other_heads(), arrive(4, 1)),
-        21: lambda: twin_sums(0),
+        13: lambda: (heads_come(), arrive(4, 1)),
+        15: lambda: other_heads(),
         18: lambda: sums((0, 1, 0), (1, 1, 1)),
         20: lambda: sums((0, 2, 1)),
-        22: lambda: sums((1, 2, 0)),
-        24: lambda: sums((0, 2, 0), (1, 2, 1)),
-        26: lambda: sums((0, 3, 1)),
-        28: lambda: sums((1, 3, 0)),
-        30: lambda: sums((0, 3, 0), (1, 3, 1)),
+        21: lambda: twin_sums(0),
+        22: lambda: sums((0, 2, 0), (1, 2, 0), (1, 2, 1)),
+        24: lambda: sums((0, 3, 1)),
+        26: lambda: sums((0, 3, 0), (1, 3, 0)),
+        28: lambda: sums((1, 3, 1)),
+        29: lambda: twin_sums(1),
+        31: lambda: (last_sum(0, 1), last_sum(0, 0), pair_sums(0)),
     }
 
     def two(i, _):
@@ -393,58 +450,62 @@
 
     lax.fori_loop(0, 32, two, 0)
 
-    twin_sums(1)
-    sums((0, 4, 1), (1, 4, 0))
-    query_sums(1, c)
-    twin_copy(1).wait_recv()
-    pair_out[...] = (dqp[1, c] + twin_in[1]).astype(BF16)
-    pair_copy = send(pair_out, pair_in, r_send.at[2], r_recv.at[2], s, pair)
-    pair_copy.start()
-    sums((0, 4, 0), (1, 4, 1))
+    last_sum(1, 0)
+    last_sum(1, 1)
+    pair_sums(1)
+
+    def own_copy(k, seq, head):
+        return send(fin.at[k], own_in.at[mine_g], b_send.at[k], b_recv.at[mine_g], seq, head)
+
+    for t in range(2):
+        value = acc[t, z].T
+        for k in range(8):
+            fin[k, t] = value[k * TILE : (k + 1) * TILE, :]
+    for k, (seq, head, other) in enumerate(givers(z)):
+        pl.when(other)(own_copy(k, seq, head).start)
+
+        @pl.when(jnp.logical_not(other))
+        def _():
+            own_in[mine_g] = fin[k]
+
     query_sums(0, c)
     twin_copy(0).wait_recv()
     dq[...] = dqp[0, c] + twin_in[0]
 
-    b_copies = []
-    g = x * 2 + y // 2
-    for t in (1, 0):
-        value = acc[t, z]
-        for way in (0, 1):
-            sum_copy(way, 4, t).wait_recv()
-            value = value + z_in[way, 3, t].astype(F32)
-        if t == 0:
-            value = value * SCALE
-        value = value.T
-        for k in range(8):
-            fin[k, t] = value[k * TILE : (k + 1) * TILE, :]
-    for k, (seq, head, other) in enumerate(givers):
-        copy = send(fin.at[k], own_in.at[g], b_send.at[k], b_recv.at[g], seq, head)
-        pl.when(other)(copy.start)
-        b_copies.append((copy, other))
-
-        @pl.when(jnp.logical_not(other))
-        def _():
-            own_in[g] = fin[k]
-
-    for g, (seq, head, other) in enumerate(takers):
+    for way in range(2):
+        for t in range(2):
+            for g, (seq, head, _) in enumerate(takers((under if way == 0 else above)[1])):
+                send(
+                    fin_way.at[way, 0, t], way_in.at[way, g, t],
+                    w_send.at[way, t, 0], w_recv.at[way, t, g], seq, head,
+                ).wait_recv()
+    for g, (seq, head, other) in enumerate(takers(z)):
         landed = send(fin.at[0], own_in.at[g], b_send.at[0], b_recv.at[g], seq, head)
         pl.when(other)(landed.wait_recv)
-    pair_copy.wait_recv()
-
-    for copy, other in a_copies + b_copies:
-        pl.when(other)(copy.wait_send)
+    for rp in range(2):
+        pair_copy(rp).wait_recv()
+
+    for o, plane in enumerate(near):
+        for g, (seq, head, other) in enumerate(takers(plane)):
+            for t in range(2):
+                pl.when(other)(row_copy(o, t, g, seq, head).wait_send)
+    for k, (seq, head, other) in enumerate(givers(z)):
+        pl.when(other)(own_copy(k, seq, head).wait_send)
     for way in range(2):
         for t in range(2):
-            for step in range(1, 5):
+            for step in range(2, 5):
                 if carries(way, step, t):
                     key_copy(way, step, t).wait_send()
+            for step in range(1, 4):
                 if step > 1 or t == way:
                     sum_copy(way, step, t).wait_send()
+            for k, (seq, head, _) in enumerate(givers((above if way == 0 else under)[1])):
+                way_copy(way, t, k, seq, head).wait_send()
     for k in range(4):
         y_copy(k).wait_send()
         if k != 2:
             forward(k).wait_send()
-    for copy in d_copies + [twin_copy(0), twin_copy(1), pair_copy]:
+    for copy in d_copies + [twin_copy(0), twin_copy(1), pair_copy(0), pair_copy(1)]:
         copy.wait_send()
 
 
@@ -460,9 +521,10 @@
             jax.ShapeDtypeStruct((ROWS, 2 * D), F32),
             jax.ShapeDtypeStruct((ROWS, 2 * D), BF16),
             jax.ShapeDtypeStruct((8, 2, TILE, D), F32),
+            jax.ShapeDtypeStruct((2, 8, 2, TILE, D), BF16),
         ),
         in_specs=[hbm] * 9,
-        out_specs=(vmem,) * 3,
+        out_specs=(vmem,) * 4,
         scratch_shapes=[
             v((TILE, 8 * D), BF16), v((TILE, 8 * D), BF16),
             v((ROWS, 2 * D), BF16), v((ROWS, 2 * D), BF16), v((ROWS, 2 * D), BF16),
@@ -481,12 +543,12 @@
             v((2, 2, ROWS, 2 * D), F32),
             v((2, ROWS, 2 * D), F32), v((ROWS, 2 * D), BF16),
             v((2, 4, 2, D, PLANE), BF16), v((2, 4, 2, D, PLANE), BF16),
-            v((8, 2, TILE, D), F32),
+            v((8, 2, TILE, D), F32), v((2, 8, 2, TILE, D), BF16),
             v((TILE, COLS), jnp.int32), v((8, D), F32),
-            dma((9,)), dma((2, 8)), dma((2, 8)),
+            dma((9,)), dma((3, 2, 8)), dma((3, 2, 8)),
             dma((2, 4, 2)), dma((2, 4, 2)), dma((2, 4, 2)), dma((2, 4, 2)),
             dma((4,)), dma((4,)), dma((3,)), dma((3,)),
-            dma((4,)), dma((4,)), dma((3,)), dma((3,)), dma((8,)), dma((8,)),
+            dma((4,)), dma((4,)), dma((4,)), dma((4,)), dma((8,)), dma((8,)), dma((2, 2, 8)), dma((2, 2, 8)),
         ],
         compiler_params=pltpu.CompilerParams(
             collective_id=0, has_side_effects=True, vmem_limit_bytes=60 * MIB
@@ -494,14 +556,15 @@
     )(keys, values, queries, grads, outs, norms, layout, ids, order)
 
 
-def finish_kernel(sums, pair_in, own_in, dq, dk, dv):
+def finish_kernel(sums, pair_in, own_in, way_in, dq, dk, dv):
     dq[...] = sums[...] + pair_in[...].astype(F32)
     for g in range(8):
-        dk[:, g * D : (g + 1) * D] = own_in[g, 0]
-        dv[:, g * D : (g + 1) * D] = own_in[g, 1]
-
-
-def finish(sums, pair_in, own_in):
+        for t, (ref, scale) in enumerate(((dk, SCALE), (dv, 1.0))):
+            total = own_in[g, t] + way_in[0, g, t].astype(F32) + way_in[1, g, t].astype(F32)
+            ref[:, g * D : (g + 1) * D] = total * scale
+
+
+def finish(sums, pair_in, own_in, way_in):
     vmem = pl.BlockSpec(memory_space=pltpu.VMEM)
     return pl.pallas_call(
         finish_kernel,
@@ -511,10 +574,10 @@
             jax.ShapeDtypeStruct((TILE, 8 * D), F32),
             jax.ShapeDtypeStruct((TILE, 8 * D), F32),
         ),
-        in_specs=[vmem] * 3,
+        in_specs=[vmem] * 4,
         out_specs=(vmem,) * 3,
         compiler_params=pltpu.CompilerParams(vmem_limit_bytes=60 * MIB),
-    )(sums, pair_in, own_in)
+    )(sums, pair_in, own_in, way_in)
 
 
 def body(

time: 69.7 us -> 69.5 us (level)
  no operation moved by 1% of the time
where the time goes in v5:
time: 69.5 us; the launch traced here: 69.4 us
  Pallas kernels  68.7 us (99%)
    pallas_call x1, Pallas kernels, fused(): pl.pallas_call(fused_kernel, name='fused', out_shape=(jax.ShapeDtypeStruc...  66.6 us
    pallas_call x1, Pallas kernels, finish(): pl.pallas_call(finish_kernel, name='finish', out_shape=(jax.ShapeDtypeStr...  2.17 us

profile of v5, /device:TPU:1, one launch (start us, length us, event | category | flops | bytes accessed | tf_op | source)
XLA Modules:
  0.0 69.4 jit_solution(5409939506750746416)
XLA Ops:
  0.6 66.6 %fused.1 = (f32[512,256]{1,0:T(8,128)}, bf16[512,256]{1,0:T(8,128)(2,1)}, f32[8,2,32,128]{3,2,1,0:T(8,128)}, bf16[2,8,2,32,128]{4,3,2,1,0:T(8,128)(2,1)}) custom-call(bf16[32,1024]{1,0:T(8,128)(2,1)} %keys_h.1, bf16[32,1024]{1,0:T(8,128)(2,1)} %values_h.1, bf16[512,256]{1,0:T(8,128)(2,1)} %queries_h.1, bf16[512,256]{1,0:T(8,128)(2,1)} %grads_h.1, ...), custom_call_target="tpu_custom_call" | custom-call | tf_op jit(solution)/shard_map/fused/pallas_call | solution.py:517
  67.2 2.2 %finish.1 = (f32[512,256]{1,0:T(8,128)}, f32[32,1024]{1,0:T(8,128)}, f32[32,1024]{1,0:T(8,128)}) custom-call(f32[512,256]{1,0:T(8,128)} %get-tuple-element.7.sums, bf16[512,256]{1,0:T(8,128)(2,1)} %get-tuple-element.8.pair_in, f32[8,2,32,128]{3,2,1,0:T(8,128)} %get-tuple-element.9.own_in, bf16[2,8,2,32,128]{4,3,2,1,0:T(8,128)(2,1)} %get-tuple-element.10.way_in), custom_call_target="tpu_custom_call" | custom-call | tf_op jit(solution)/shard_map/finish/pallas_call | solution.py:569

commit v6 on v5

--- a/solution.py
+++ b/solution.py
@@ -64,12 +64,12 @@
 
 def fused_kernel(
     keys_h, values_h, queries_h, grads_h, outs_h, norms_h, layout_h, ids_h, order_h,
-    dq, pair_in, own_in, way_in,
+    dq, pair_in, way_in,
     keys, values, queries, grads, outs, norms, layout, ids, order, order_v,
     kv, qt, gt, st, lay, l_in, lperm, spans, docs,
-    ax, qx, gx, lows, sgs, acc, dqt, dqp, twin_in, pair_out, z_out, z_in, fin, fin_way, ahead, pick,
+    ax, qx, gx, lows, sgs, acc, dqt, dqp, twin_in, pair_out, z_out, z_in, fin, ahead, pick,
     l_sem, a_send, a_recv, k_send, k_recv, z_send, z_recv, y_send, y_recv, d_send, d_recv,
-    f_send, f_recv, r_send, r_recv, b_send, b_recv, w_send, w_recv,
+    f_send, f_recv, r_send, r_recv, w_send, w_recv,
 ):
     s, h, z, c, x, y = place()
     pair = h + 1 - 2 * (y % 2)
@@ -371,7 +371,7 @@
 
     def way_copy(way, t, k, seq, head):
         return send(
-            fin_way.at[way, k, t], way_in.at[way, mine_g, t],
+            fin.at[way, k, t], way_in.at[way, mine_g, t],
             w_send.at[way, t, k], w_recv.at[way, t, mine_g], seq, head,
         )
 
@@ -380,7 +380,7 @@
         sum_copy(way, 3, t).wait_recv()
         value = (acc[t, plane] + z_in[way, 2, t].astype(F32)).T.astype(BF16)
         for k, (seq, head, _) in enumerate(givers(plane)):
-            fin_way[way, k, t] = value[k * TILE : (k + 1) * TILE, :]
+            fin[way, k, t] = value[k * TILE : (k + 1) * TILE, :]
         for k, (seq, head, _) in enumerate(givers(plane)):
             way_copy(way, t, k, seq, head).start()
 
@@ -439,8 +439,14 @@
     }
 
     def two(i, _):
-        for at, event in events.items():
-            pl.when(i == at)(lambda event=event: (event(), None)[1])
+        def happen(steps):
+            if len(steps) == 1:
+                pl.when(i == steps[0])(lambda: (events[steps[0]](), None)[1])
+            else:
+                mid = len(steps) // 2
+                lax.cond(i < steps[mid], lambda: happen(steps[:mid]), lambda: happen(steps[mid:]))
+
+        happen(sorted(events))
         n = 2 * i
         lows[1], sgs[1] = front(n + 1)
         back(n, lows[0], sgs[0])
@@ -454,34 +460,29 @@
     last_sum(1, 1)
     pair_sums(1)
 
-    def own_copy(k, seq, head):
-        return send(fin.at[k], own_in.at[mine_g], b_send.at[k], b_recv.at[mine_g], seq, head)
-
     for t in range(2):
-        value = acc[t, z].T
+        value = acc[t, z].T.astype(BF16)
         for k in range(8):
-            fin[k, t] = value[k * TILE : (k + 1) * TILE, :]
-    for k, (seq, head, other) in enumerate(givers(z)):
-        pl.when(other)(own_copy(k, seq, head).start)
-
-        @pl.when(jnp.logical_not(other))
-        def _():
-            own_in[mine_g] = fin[k]
+            fin[2, k, t] = value[k * TILE : (k + 1) * TILE, :]
+        for k, (seq, head, other) in enumerate(givers(z)):
+            pl.when(other)(way_copy(2, t, k, seq, head).start)
+
+            @pl.when(jnp.logical_not(other))
+            def _():
+                way_in[2, mine_g, t] = fin[2, k, t]
 
     query_sums(0, c)
     twin_copy(0).wait_recv()
     dq[...] = dqp[0, c] + twin_in[0]
 
-    for way in range(2):
+    for way, plane in enumerate((under[1], above[1], z)):
         for t in range(2):
-            for g, (seq, head, _) in enumerate(takers((under if way == 0 else above)[1])):
-                send(
-                    fin_way.at[way, 0, t], way_in.at[way, g, t],
+            for g, (seq, head, other) in enumerate(takers(plane)):
+                landed = send(
+                    fin.at[way, 0, t], way_in.at[way, g, t],
                     w_send.at[way, t, 0], w_recv.at[way, t, g], seq, head,
-                ).wait_recv()
-    for g, (seq, head, other) in enumerate(takers(z)):
-        landed = send(fin.at[0], own_in.at[g], b_send.at[0], b_recv.at[g], seq, head)
-        pl.when(other)(landed.wait_recv)
+                )
+                pl.when(other)(landed.wait_recv)
     for rp in range(2):
         pair_copy(rp).wait_recv()
 
@@ -489,8 +490,10 @@
         for g, (seq, head, other) in enumerate(takers(plane)):
             for t in range(2):
                 pl.when(other)(row_copy(o, t, g, seq, head).wait_send)
-    for k, (seq, head, other) in enumerate(givers(z)):
-        pl.when(other)(own_copy(k, seq, head).wait_send)
+    for way, plane in enumerate((above[1], under[1], z)):
+        for t in range(2):
+            for k, (seq, head, other) in enumerate(givers(plane)):
+                pl.when(other)(way_copy(way, t, k, seq, head).wait_send)
     for way in range(2):
         for t in range(2):
             for step in range(2, 5):
@@ -499,8 +502,6 @@
             for step in range(1, 4):
                 if step > 1 or t == way:
                     sum_copy(way, step, t).wait_send()
-            for k, (seq, head, _) in enumerate(givers((above if way == 0 else under)[1])):
-                way_copy(way, t, k, seq, head).wait_send()
     for k in range(4):
         y_copy(k).wait_send()
         if k != 2:
@@ -520,11 +521,10 @@
         out_shape=(
             jax.ShapeDtypeStruct((ROWS, 2 * D), F32),
             jax.ShapeDtypeStruct((ROWS, 2 * D), BF16),
-            jax.ShapeDtypeStruct((8, 2, TILE, D), F32),
-            jax.ShapeDtypeStruct((2, 8, 2, TILE, D), BF16),
+            jax.ShapeDtypeStruct((3, 8, 2, TILE, D), BF16),
         ),
         in_specs=[hbm] * 9,
-        out_specs=(vmem,) * 4,
+        out_specs=(vmem,) * 3,
         scratch_shapes=[
             v((TILE, 8 * D), BF16), v((TILE, 8 * D), BF16),
             v((ROWS, 2 * D), BF16), v((ROWS, 2 * D), BF16), v((ROWS, 2 * D), BF16),
@@ -543,12 +543,12 @@
             v((2, 2, ROWS, 2 * D), F32),
             v((2, ROWS, 2 * D), F32), v((ROWS, 2 * D), BF16),
             v((2, 4, 2, D, PLANE), BF16), v((2, 4, 2, D, PLANE), BF16),
-            v((8, 2, TILE, D), F32), v((2, 8, 2, TILE, D), BF16),
+            v((3, 8, 2, TILE, D), BF16),
             v((TILE, COLS), jnp.int32), v((8, D), F32),
             dma((9,)), dma((3, 2, 8)), dma((3, 2, 8)),
             dma((2, 4, 2)), dma((2, 4, 2)), dma((2, 4, 2)), dma((2, 4, 2)),
             dma((4,)), dma((4,)), dma((3,)), dma((3,)),
-            dma((4,)), dma((4,)), dma((4,)), dma((4,)), dma((8,)), dma((8,)), dma((2, 2, 8)), dma((2, 2, 8)),
+            dma((4,)), dma((4,)), dma((4,)), dma((4,)), dma((3, 2, 8)), dma((3, 2, 8)),
         ],
         compiler_params=pltpu.CompilerParams(
             collective_id=0, has_side_effects=True, vmem_limit_bytes=60 * MIB
@@ -556,15 +556,15 @@
     )(keys, values, queries, grads, outs, norms, layout, ids, order)
 
 
-def finish_kernel(sums, pair_in, own_in, way_in, dq, dk, dv):
+def finish_kernel(sums, pair_in, way_in, dq, dk, dv):
     dq[...] = sums[...] + pair_in[...].astype(F32)
     for g in range(8):
         for t, (ref, scale) in enumerate(((dk, SCALE), (dv, 1.0))):
-            total = own_in[g, t] + way_in[0, g, t].astype(F32) + way_in[1, g, t].astype(F32)
+            total = way_in[2, g, t].astype(F32) + way_in[0, g, t].astype(F32) + way_in[1, g, t].astype(F32)
             ref[:, g * D : (g + 1) * D] = total * scale
 
 
-def finish(sums, pair_in, own_in, way_in):
+def finish(sums, pair_in, way_in):
     vmem = pl.BlockSpec(memory_space=pltpu.VMEM)
     return pl.pallas_call(
         finish_kernel,
@@ -574,10 +574,10 @@
             jax.ShapeDtypeStruct((TILE, 8 * D), F32),
             jax.ShapeDtypeStruct((TILE, 8 * D), F32),
         ),
-        in_specs=[vmem] * 4,
+        in_specs=[vmem] * 3,
         out_specs=(vmem,) * 3,
         compiler_params=pltpu.CompilerParams(vmem_limit_bytes=60 * MIB),
-    )(sums, pair_in, own_in, way_in)
+    )(sums, pair_in, way_in)
 
 
 def body(

time: 69.5 us -> 66.9 us (0.963)
  Pallas kernels: 68.7 us -> 66.1 us
    pallas_call x1, Pallas kernels: 66.6 us -> 64 us  [fused(): pl.pallas_call(fused_kernel, name='fused', out_shape=(jax.ShapeDtypeStruc...]
where the time goes in v6:
time: 66.9 us; the launch traced here: 66.8 us
  Pallas kernels  66.1 us (99%)
    pallas_call x1, Pallas kernels, fused(): pl.pallas_call(fused_kernel, name='fused', out_shape=(jax.ShapeDtypeStruc...  64 us
    pallas_call x1, Pallas kernels, finish(): pl.pallas_call(finish_kernel, name='finish', out_shape=(jax.ShapeDtypeStr...  2.14 us

profile of v6, /device:TPU:1, one launch (start us, length us, event | category | flops | bytes accessed | tf_op | source)
XLA Modules:
  0.0 66.8 jit_solution(1569012668784912979)
XLA Ops:
  0.6 64.0 %fused.1 = (f32[512,256]{1,0:T(8,128)}, bf16[512,256]{1,0:T(8,128)(2,1)}, bf16[3,8,2,32,128]{4,3,2,1,0:T(8,128)(2,1)}) custom-call(bf16[32,1024]{1,0:T(8,128)(2,1)} %keys_h.1, bf16[32,1024]{1,0:T(8,128)(2,1)} %values_h.1, bf16[512,256]{1,0:T(8,128)(2,1)} %queries_h.1, bf16[512,256]{1,0:T(8,128)(2,1)} %grads_h.1, bf16[512,256]{1,0:T(8,128)(2,1)} %outs_h.1, ...), custom_call_target="tpu_custom_call" | custom-call | tf_op jit(solution)/shard_map/fused/pallas_call | solution.py:518
  64.7 2.1 %finish.1 = (f32[512,256]{1,0:T(8,128)}, f32[32,1024]{1,0:T(8,128)}, f32[32,1024]{1,0:T(8,128)}) custom-call(f32[512,256]{1,0:T(8,128)} %get-tuple-element.6.sums, bf16[512,256]{1,0:T(8,128)(2,1)} %get-tuple-element.7.pair_in, bf16[3,8,2,32,128]{4,3,2,1,0:T(8,128)(2,1)} %get-tuple-element.8.way_in), custom_call_target="tpu_custom_call" | custom-call | tf_op jit(solution)/shard_map/finish/pallas_call | solution.py:569

commit v7 on v6

--- a/solution.py
+++ b/solution.py
@@ -113,7 +113,7 @@
     for seq, head in ((s, pair), (twin, h), (up, h), (down, h)):
         pl.semaphore_signal(barrier, inc=1, device_id=(seq, head), device_id_type=MESH)
     for plane in near:
-        for seq, head, other in takers(plane) + givers(plane):
+        for seq, head, other in givers(plane):
 
             @pl.when(other)
             def _():
@@ -133,7 +133,7 @@
     for load in loads[1:4]:
         load.wait()
     columns(grads, gt)
-    pl.semaphore_wait(barrier, 4 + 48 - 2 * own)
+    pl.semaphore_wait(barrier, 4 + 24 - own)
 
     slot = c * 4 + x
     slot_rows = pl.ds(pl.multiple_of(slot * TILE, TILE), TILE)
@@ -438,23 +438,30 @@
         31: lambda: (last_sum(0, 1), last_sum(0, 0), pair_sums(0)),
     }
 
-    def two(i, _):
-        def happen(steps):
-            if len(steps) == 1:
-                pl.when(i == steps[0])(lambda: (events[steps[0]](), None)[1])
-            else:
-                mid = len(steps) // 2
-                lax.cond(i < steps[mid], lambda: happen(steps[:mid]), lambda: happen(steps[mid:]))
-
-        happen(sorted(events))
+    def pair_of_steps(i):
         n = 2 * i
         lows[1], sgs[1] = front(n + 1)
         back(n, lows[0], sgs[0])
         lows[0], sgs[0] = front(jnp.minimum(n + 2, 63))
         back(n + 1, lows[1], sgs[1])
-        return 0
-
-    lax.fori_loop(0, 32, two, 0)
+
+    def happen(i, steps):
+        if len(steps) == 1:
+            pl.when(i == steps[0])(lambda: (events[steps[0]](), None)[1])
+        else:
+            mid = len(steps) // 2
+            lax.cond(i < steps[mid], lambda: happen(i, steps[:mid]), lambda: happen(i, steps[mid:]))
+
+    def steps_between(lo, hi):
+        def two(i, _):
+            happen(i, [at for at in sorted(events) if lo <= at < hi])
+            pair_of_steps(i)
+            return 0
+
+        lax.fori_loop(lo, hi, two, 0)
+
+    steps_between(0, 16)
+    steps_between(16, 32)
 
     last_sum(1, 0)
     last_sum(1, 1)

time: 66.9 us -> 66.4 us (level)
  no operation moved by 1% of the time
where the time goes in v7:
time: 66.4 us; the launch traced here: 66.2 us
  Pallas kernels  65.6 us (99%)
    pallas_call x1, Pallas kernels, fused(): pl.pallas_call(fused_kernel, name='fused', out_shape=(jax.ShapeDtypeStruc...  63.5 us
    pallas_call x1, Pallas kernels, finish(): pl.pallas_call(finish_kernel, name='finish', out_shape=(jax.ShapeDtypeStr...  2.14 us

profile of v7, /device:TPU:1, one launch (start us, length us, event | category | flops | bytes accessed | tf_op | source)
XLA Modules:
  0.0 66.2 jit_solution(3351810119741546843)
XLA Ops:
  0.6 63.5 %fused.1 = (f32[512,256]{1,0:T(8,128)}, bf16[512,256]{1,0:T(8,128)(2,1)}, bf16[3,8,2,32,128]{4,3,2,1,0:T(8,128)(2,1)}) custom-call(bf16[32,1024]{1,0:T(8,128)(2,1)} %keys_h.1, bf16[32,1024]{1,0:T(8,128)(2,1)} %values_h.1, bf16[512,256]{1,0:T(8,128)(2,1)} %queries_h.1, bf16[512,256]{1,0:T(8,128)(2,1)} %grads_h.1, bf16[512,256]{1,0:T(8,128)(2,1)} %outs_h.1, ...), custom_call_target="tpu_custom_call" | custom-call | tf_op jit(solution)/shard_map/fused/pallas_call | solution.py:525
  64.1 2.1 %finish.1 = (f32[512,256]{1,0:T(8,128)}, f32[32,1024]{1,0:T(8,128)}, f32[32,1024]{1,0:T(8,128)}) custom-call(f32[512,256]{1,0:T(8,128)} %get-tuple-element.6.sums, bf16[512,256]{1,0:T(8,128)(2,1)} %get-tuple-element.7.pair_in, bf16[3,8,2,32,128]{4,3,2,1,0:T(8,128)(2,1)} %get-tuple-element.8.way_in), custom_call_target="tpu_custom_call" | custom-call | tf_op jit(solution)/shard_map/finish/pallas_call | solution.py:576
